TPU v7x, 32 devices: a whole 2x2x4 slice. The times are simulated.
32 devices in a mesh: seq: 8 (over z, y), grp: 4 (over x, core).
Axes of the slice: x: 2, y: 2, z: 4, core: 2. Of those that a mesh axis runs over, the one named last changes fastest.
Arguments:
- hidden: bfloat16 [4096, 2048], P('seq', 'grp'), may hold values from -8 to 8
- qkv_weight: bfloat16 [3, 2048, 6144], P(None, 'seq', 'grp'), may hold values from -0.125 to 0.125
- out_weight: bfloat16 [3, 2048, 2048], P(None, 'grp', 'seq'), may hold values from -0.125 to 0.125
- projection: float32 [3, 16, 128, 128], P(None, 'grp'), may hold values from -6 to 6
- norm_gain: float32 [3, 2048], replicated, may hold values from 0.1 to 1.9
- out_gain: float32 [3, 2048], P(None, 'grp'), may hold values from 0.1 to 1.9
Outputs:
- layer_out: bfloat16 [4096, 2048], P('seq', 'grp')
All inputs are finite; a program needn't handle non-finite values.
Results may differ from a plain program's by a relative error of at most 0.034.
Values may be sent and summed in bfloat16 or wider, within the bound.
A program may use at most 64 MiB of HBM per device.

v0:
```python
import functools
import math

import jax
import jax.numpy as jnp
from jax import lax
from jax.experimental import pallas as pl
from jax.experimental.pallas import tpu as pltpu
from jax.sharding import PartitionSpec as P

MESH = pl.DeviceIdType.MESH
stabilizer = 2.0
f32 = jnp.float32
bf16 = jnp.bfloat16


def remote(src, dst, send, recv, device):
    return pltpu.make_async_remote_copy(
        src_ref=src, dst_ref=dst, send_sem=send, recv_sem=recv, device_id=device, device_id_type=MESH
    )


def exchange(line, step, lines):
    if lines & (lines - 1):
        return lax.rem(line + step, lines), lax.rem(line + lines - step, lines)
    other, bit = line, 1
    while bit < lines:
        if step & bit:
            other = other + bit * (1 - 2 * ((line // bit) % 2))
        bit *= 2
    return other, other


def kernel(
    n_seq, n_grp, hidden, qkv_w, out_w, proj, norm_gain, out_gain, out,
    wq, wo, xg, part, rs, normed, qf, kf, vf, num, den, att,
    own_state, st_send, st_pair, ps_send, st_line, prefix,
    local_sem, z_send, z_recv, y_send, y_recv, p_send, p_recv, l_send, l_recv,
    ag_send, ag_recv, rs_send, rs_recv,
):
    layers, rows, cols = qkv_w.shape
    oc = out_w.shape[2]
    tokens, width = hidden.shape
    heads = proj.shape[1]
    head = proj.shape[2]
    feats = proj.shape[3] // 3
    lines = n_seq // 2
    me = lax.axis_index("seq")
    grp = lax.axis_index("grp")
    line, parity = me // 2, me % 2
    pair = line * 2 + 1 - parity

    stores = ((qkv_w, wq), (out_w, wo))
    halves = 2
    cut_rows = rows // halves

    def piece(l, k, owner):
        if k == halves:
            return wo.at[l, owner]
        return wq.at[l, owner, pl.ds(k * cut_rows, cut_rows)]

    own_copies = [
        [pltpu.make_async_copy(src.at[l], dst.at[l, me], local_sem.at[1 + 2 * l + k]) for k, (src, dst) in enumerate(stores)]
        for l in range(layers)
    ]
    own_hidden = pltpu.make_async_copy(hidden, xg.at[grp], local_sem.at[0])
    own_hidden.start()
    for pair_copies in own_copies:
        for c in pair_copies:
            c.start()

    barrier = pltpu.get_barrier_semaphore()
    for k in range(1, lines):
        pl.semaphore_signal(barrier, inc=1, device_id={"seq": lax.rem(line + k, lines) * 2 + parity}, device_id_type=MESH)
    pl.semaphore_signal(barrier, inc=1, device_id={"seq": pair}, device_id_type=MESH)
    for k in range(1, n_grp):
        pl.semaphore_signal(barrier, inc=1, device_id={"grp": lax.rem(grp + k, n_grp)}, device_id_type=MESH)
    pl.semaphore_wait(barrier, lines + n_grp - 1)

    def z_copy(l, k, step):
        ref = piece(l, k, me)
        to = exchange(line, step, lines)[0] * 2 + parity
        return remote(ref, ref, z_send.at[l, k, step], z_recv.at[l, k, line], {"seq": to})

    def z_arrival(l, k, step):
        src = exchange(line, step, lines)[1]
        ref = piece(l, k, src * 2 + parity)
        return remote(ref, ref, z_send.at[l, k, step], z_recv.at[l, k, src], {"seq": src * 2 + parity})

    def y_copy(l, k, step):
        src = exchange(line, step, lines)[1]
        ref = piece(l, k, src * 2 + parity)
        return remote(ref, ref, y_send.at[l, k, src], y_recv.at[l, k, src], {"seq": pair})

    def y_arrival(l, k, step):
        src = exchange(line, step, lines)[1]
        ref = piece(l, k, src * 2 + 1 - parity)
        return remote(ref, ref, y_send.at[l, k, src], y_recv.at[l, k, src], {"seq": pair})

    order = list(range(1, lines))
    arrivals = [(k, step) for k in range(halves) for step in order]

    def send_weights(l):
        for c in own_copies[l]:
            c.wait()
        for k in range(halves + 1):
            for step in order:
                z_copy(l, k, step).start()

    def pair_weights(l):
        for k in range(halves + 1):
            y_copy(l, k, 0).start()

    def forward(l, k, step):
        z_arrival(l, k, step).wait_recv()
        y_copy(l, k, step).start()

    def ag_copy(l, k):
        to = lax.rem(grp + k, n_grp)
        return remote(xg.at[grp], xg.at[grp], ag_send.at[l, k], ag_recv.at[l, grp], {"grp": to})

    def ag_arrival(l, k):
        src = lax.rem(grp + k, n_grp)
        return remote(xg.at[src], xg.at[src], ag_send.at[l, k], ag_recv.at[l, src], {"grp": src})

    def rs_copy(l, k):
        to = lax.rem(grp + k, n_grp)
        return remote(part.at[to], rs.at[grp], rs_send.at[l, k], rs_recv.at[l, grp], {"grp": to})

    def rs_arrival(l, k):
        src = lax.rem(grp + k, n_grp)
        return remote(part.at[src], rs.at[src], rs_send.at[l, k], rs_recv.at[l, src], {"grp": src})

    def pair_copy(l):
        return remote(st_send.at[l], st_pair.at[l], p_send.at[l], p_recv.at[l], {"seq": pair})

    def line_copy(l, step):
        return remote(
            ps_send.at[l], st_line.at[l, line], l_send.at[l, step], l_recv.at[l, line],
            {"seq": lax.rem(line + step, lines) * 2 + parity},
        )

    def line_arrival(l, step):
        src = lax.rem(line + lines - step, lines)
        return remote(ps_send.at[l], st_line.at[l, src], l_send.at[l, step], l_recv.at[l, src], {"seq": src * 2 + parity})

    own_hidden.wait()
    for k in range(1, n_grp):
        ag_copy(0, k).start()
    send_weights(0)
    pair_weights(0)

    scale = head ** (-0.25)
    inv = 1.0 / math.sqrt(feats)

    def features(u, terms):
        mixed = jnp.dot(u, terms, preferred_element_type=f32)
        mixed = (mixed[:, 2 * feats :] + mixed[:, feats : 2 * feats]) + mixed[:, :feats]
        w0 = u.astype(f32) * scale
        energy = 0.5 * jnp.sum(w0 * w0, axis=-1, keepdims=True)
        return (jnp.exp(mixed - energy - stabilizer) * inv).astype(bf16)

    forwarded = 0
    for l in range(layers):
        last = l == layers - 1
        for k in range(1, n_grp):
            ag_copy(l, k).wait_send()
            ag_arrival(l, k).wait_recv()

        @pl.loop(0, tokens // 64)
        def _(t):
            at = pl.ds(pl.multiple_of(t * 64, 64), 64)
            wide = [xg[g, at, :].astype(f32) for g in range(n_grp)]
            total = sum(jnp.sum(v * v, axis=-1, keepdims=True) for v in wide)
            rms = lax.rsqrt(total / (width * n_grp) + 1e-05)
            for g in range(n_grp):
                cut = slice(g * width, (g + 1) * width)
                normed[at, cut] = (wide[g] * rms * norm_gain[l : l + 1, cut]).astype(bf16)

        for k, step in arrivals[forwarded:]:
            forward(l, k, step)
        for k in range(halves):
            for step in range(lines):
                y_arrival(l, k, step).wait_recv()

        @pl.loop(0, heads)
        def _(h):
            at = pl.ds(pl.multiple_of(h * 3 * head, 128), 3 * head)
            w = wq[l, :, :, at].reshape(n_seq * rows, 3 * head)
            qkv = jnp.dot(normed[...], w, preferred_element_type=f32).astype(bf16)
            terms = proj[l, h]
            key = features(qkv[:, head : 2 * head], terms)
            value = qkv[:, 2 * head :]
            qf[h] = features(qkv[:, :head], terms)
            kf[h] = key
            vf[h] = value
            kv = lax.dot_general(key, value, (((0,), (0,)), ((), ())), preferred_element_type=f32)
            z = jnp.dot(jnp.ones((16, tokens), bf16), key, preferred_element_type=f32)
            own_state[h, :feats] = kv
            own_state[h, feats:] = z
            st_send[l, h, :feats] = kv.astype(bf16)
            st_send[l, h, feats:] = z.astype(bf16)

        pair_copy(l).start()
        pair_copy(l).wait_recv()

        @pl.loop(0, heads)
        def _(h):
            ps_send[l, h] = (own_state[h] + st_pair[l, h].astype(f32)).astype(bf16)

        for step in range(1, lines):
            @pl.when(line + step < lines)
            def _(step=step):
                line_copy(l, step).start()

        if not last:
            send_weights(l + 1)
        for step in order:
            forward(l, halves, step)
        if not last:
            pair_weights(l + 1)

        @pl.loop(0, heads)
        def _(h):
            scores = lax.dot_general(qf[h], kf[h], (((1,), (1,)), ((), ())), preferred_element_type=f32)
            r = lax.broadcasted_iota(jnp.int32, (tokens, tokens), 0)
            c = lax.broadcasted_iota(jnp.int32, (tokens, tokens), 1)
            masked = jnp.where(r >= c, scores, 0.0)
            den[h] = jnp.broadcast_to(jnp.sum(masked, axis=-1, keepdims=True), (tokens, head))
            num[h] = jnp.dot(masked.astype(bf16), vf[h], preferred_element_type=f32)

        odd = jnp.where(parity == 1, 1.0, 0.0)

        @pl.loop(0, heads)
        def _(h):
            prefix[h] = st_pair[l, h].astype(f32) * odd

        for step in range(1, lines):
            @pl.when(line >= step)
            def _(step=step):
                line_arrival(l, step).wait_recv()
                src = lax.rem(line + lines - step, lines)

                @pl.loop(0, heads)
                def _(h):
                    prefix[h] = prefix[h] + st_line[l, src, h].astype(f32)

        @pl.loop(0, heads)
        def _(h):
            q = qf[h]
            z = prefix[h, feats : feats + 1]
            d = den[h] + jnp.sum(q.astype(f32) * z, axis=-1, keepdims=True)
            n = num[h] + jnp.dot(q, prefix[h, :feats].astype(bf16), preferred_element_type=f32)
            a = n / d
            norm = lax.rsqrt(jnp.mean(a * a, axis=-1, keepdims=True) + 1e-06)
            att[:, pl.ds(pl.multiple_of(h * head, 128), head)] = (a * norm * out_gain[l, h]).astype(bf16)

        for step in range(lines):
            y_arrival(l, halves, step).wait_recv()
        per = width // oc
        for k in list(range(1, n_grp)) + [0]:
            to = lax.rem(grp + k, n_grp)
            for i in range(per):
                part[to, :, i * oc : (i + 1) * oc] = jnp.dot(
                    att[...], wo[l, to * per + i], preferred_element_type=f32
                ).astype(bf16)
            if k:
                rs_copy(l, k).start()
        forwarded = 0
        if not last and lines > 1:
            forwarded = min(2, len(arrivals))
            for k, step in arrivals[:forwarded]:
                forward(l + 1, k, step)
        for k in range(1, n_grp):
            rs_copy(l, k).wait_send()
            rs_arrival(l, k).wait_recv()

        @pl.loop(0, tokens // 64)
        def _(t):
            at = pl.ds(pl.multiple_of(t * 64, 64), 64)
            total = part[grp, at, :].astype(f32)
            for k in range(1, n_grp):
                total = total + rs[lax.rem(grp + k, n_grp), at, :].astype(f32)
            total = (xg[grp, at, :].astype(f32) + total).astype(bf16)
            if last:
                out[at, :] = total
            else:
                xg[grp, at, :] = total

        if not last:
            for k in range(1, n_grp):
                ag_copy(l + 1, k).start()
            ready = min(4, len(arrivals))
            for k, step in arrivals[forwarded:ready]:
                forward(l + 1, k, step)
            forwarded = ready

    for l in range(layers):
        pair_copy(l).wait_send()
        for k in range(halves + 1):
            for step in range(1, lines):
                z_copy(l, k, step).wait_send()
            for step in range(lines):
                y_copy(l, k, step).wait_send()
        for step in range(1, lines):
            @pl.when(line + step < lines)
            def _(step=step):
                line_copy(l, step).wait_send()


def local(n_seq, n_grp, hidden, qkv_weight, out_weight, projection, norm_gain, out_gain):
    layers, rows, cols = qkv_weight.shape
    depth, oc = out_weight.shape[1:]
    heads, head, feats = projection.shape[1:]
    tokens, width = hidden.shape
    lines = n_seq // 2
    scaled = projection * head ** (-0.25)
    high = lax.reduce_precision(scaled, 8, 7)
    rest = scaled - high
    mid = lax.reduce_precision(rest, 8, 7)
    low = rest - mid
    terms = jnp.concatenate([high, mid, low], axis=-1).astype(bf16)
    gains = out_gain.reshape(layers, heads, 1, head)
    dma = pltpu.SemaphoreType.DMA
    vmem = pl.BlockSpec(memory_space=pltpu.VMEM)
    anywhere = pl.BlockSpec(memory_space=pl.ANY)
    state = (heads, feats + 16, head)
    return pl.pallas_call(
        functools.partial(kernel, n_seq, n_grp),
        out_shape=jax.ShapeDtypeStruct((tokens, width), bf16),
        in_specs=[anywhere, anywhere, anywhere, vmem, vmem, vmem],
        out_specs=vmem,
        scratch_shapes=[
            pltpu.VMEM((layers, n_seq, rows, cols), bf16),
            pltpu.VMEM((layers, n_seq, depth, oc), bf16),
            pltpu.VMEM((n_grp, tokens, width), bf16),
            pltpu.VMEM((n_grp, tokens, width), bf16),
            pltpu.VMEM((n_grp, tokens, width), bf16),
            pltpu.VMEM((tokens, n_grp * width), bf16),
            pltpu.VMEM((heads, tokens, feats), bf16),
            pltpu.VMEM((heads, tokens, feats), bf16),
            pltpu.VMEM((heads, tokens, head), bf16),
            pltpu.VMEM((heads, tokens, head), f32),
            pltpu.VMEM((heads, tokens, head), f32),
            pltpu.VMEM((tokens, heads * head), bf16),
            pltpu.VMEM(state, f32),
            pltpu.VMEM((layers,) + state, bf16),
            pltpu.VMEM((layers,) + state, bf16),
            pltpu.VMEM((layers,) + state, bf16),
            pltpu.VMEM((layers, lines) + state, bf16),
            pltpu.VMEM(state, f32),
            dma((1 + 2 * layers,)),
            dma((layers, 3, lines)),
            dma((layers, 3, lines)),
            dma((layers, 3, lines)),
            dma((layers, 3, lines)),
            dma((layers,)),
            dma((layers,)),
            dma((layers, lines)),
            dma((layers, lines)),
            dma((layers, n_grp)),
            dma((layers, n_grp)),
            dma((layers, n_grp)),
            dma((layers, n_grp)),
        ],
        compiler_params=pltpu.CompilerParams(
            collective_id=0, has_side_effects=True, vmem_limit_bytes=66_000_000
        ),
    )(hidden, qkv_weight, out_weight, terms, norm_gain, gains)


def solution(mesh):
    return jax.shard_map(
        functools.partial(local, mesh.shape["seq"], mesh.shape["grp"]),
        mesh=mesh,
        in_specs=(
            P("seq", "grp"),
            P(None, "seq", "grp"),
            P(None, "grp", "seq"),
            P(None, "grp", None, None),
            P(),
            P(None, "grp"),
        ),
        out_specs=P("seq", "grp"),
        check_vma=False,
    )
```

profile of v0, /device:TPU:23, one launch (start us, length us, event | category | flops | bytes accessed | tf_op | source)
XLA Modules:
  0.0 362.2 jit_solution(1192471039272497922)
XLA Ops:
  0.0 0.0 copy-start
  0.0 1.5 reduce-precision_convert_fusion.1
  1.5 1.2 pad_maximum_fusion.proj
  2.7 0.0 copy-done
  2.7 0.6 reshape.3.out_gain
  3.3 357.1 %shard_map.64 = bf16[512,512]{1,0:T(8,128)(2,1)} custom-call(bf16[512,512]{1,0:T(8,128)(2,1)} %hidden.1, bf16[3,256,1536]{2,1,0:T(8,128)(2,1)} %qkv_w.1, bf16[3,512,256]{2,1,0:T(8,128)(2,1)} %out_w.1, bf16[3,4,128,384]{3,2,1,0:T(8,128)(2,1)} %pad_maximum_fusion.proj, f32[3,2048]{1,0:T(4,128)} %norm_gain.1, f32[3,4,1,128]{3,2,1,0:T(1,128)} %reshape.3.out_gain), custom_call_target="tpu_custom_call" | custom-call | tf_op jit(solution)/shard_map/pallas_call | solution.py:328
  360.4 1.9 copy.8
Async XLA Ops:
  0.0 2.7 copy-start
where the time goes:
time: 362 us
  Pallas kernels  357 us (99%)
    pallas_call x1, Pallas kernels, local(): pl.pallas_call(functools.partial(kernel, n_seq, n_grp), out_shape=jax.Sha...  357 us

commit v1 on v0

v1 whole, which is shorter than its diff:
```python
import functools
import math

import jax
import jax.numpy as jnp
from jax import lax
from jax.experimental import pallas as pl
from jax.experimental.pallas import tpu as pltpu
from jax.sharding import PartitionSpec as P

MESH = pl.DeviceIdType.MESH
stabilizer = 2.0
f32 = jnp.float32
bf16 = jnp.bfloat16


def remote(src, dst, send, recv, device):
    return pltpu.make_async_remote_copy(
        src_ref=src, dst_ref=dst, send_sem=send, recv_sem=recv, device_id=device, device_id_type=MESH
    )


def kernel(
    n_seq, n_grp, hidden, qkv_w, out_w, proj, norm_gain, out_gain, out,
    wq, wo, xg, part, rsd, rx, ry, rv, ru, ub, vb, normed, qf, kf, vf, num, den, att,
    own_state, st_send, st_line, prefix,
    local_sem, z_send, z_recv, r_send, y_send, y_recv, l_send, l_recv,
    ag_send, ag_recv, d_send, d_recv, x_send, x_recv, w_send, w_recv, u_send, u_recv, v_send, v_recv,
):
    layers, rows, cols = qkv_w.shape
    depth, oc = out_w.shape[1:]
    tokens, width = hidden.shape
    heads, head = proj.shape[1:3]
    feats = proj.shape[3] // 3
    lines = n_seq // 2
    chips = n_grp // 2
    mine = heads // 2
    half = tokens // 2
    step_rows = 64
    me = lax.axis_index("seq")
    grp = lax.axis_index("grp")
    line, parity = me // 2, me % 2
    other = 1 - parity
    pair = line * 2 + other
    chip, core = grp // 2, grp % 2
    partner = chip * 2 + 1 - core

    def chip_at(j):
        return lax.rem(chip + j, chips)

    def beside(j):
        return chip_at(j) * 2 + core

    def piece(h):
        return pl.ds(h * half, half)

    def weight(l, k, slot):
        return (wo if k else wq).at[l, slot]

    def own_part(l, k, who):
        if k:
            return out_w.at[l, pl.ds(pl.multiple_of(who * (depth // 2), depth // 2), depth // 2)]
        return qkv_w.at[l, :, pl.ds(pl.multiple_of(who * (cols // 2), cols // 2), cols // 2)]

    own_copies = [
        [pltpu.make_async_copy(own_part(l, k, parity), weight(l, k, me), local_sem.at[1 + 2 * l + k]) for k in range(2)]
        for l in range(layers)
    ]
    own_hidden = pltpu.make_async_copy(hidden, xg.at[parity, grp], local_sem.at[0])
    own_hidden.start()
    for both in own_copies:
        for c in both:
            c.start()

    barrier = pltpu.get_barrier_semaphore()
    for k in range(1, lines):
        pl.semaphore_signal(barrier, inc=1, device_id={"seq": lax.rem(line + k, lines) * 2 + parity}, device_id_type=MESH)
    pl.semaphore_signal(barrier, inc=1, device_id={"seq": pair}, device_id_type=MESH)
    for k in range(1, n_grp):
        pl.semaphore_signal(barrier, inc=1, device_id={"grp": lax.rem(grp + k, n_grp)}, device_id_type=MESH)
    pl.semaphore_wait(barrier, lines + n_grp - 1)

    reach = max(1, lines - 2)
    relays = ((lines - 2, 0, lines - 1), (1, lines - 1, 0)) if lines > 2 else ()

    def slot_of(where, side):
        return where * 2 + (other if side else parity)

    def y_copy(l, k):
        return remote(own_part(l, k, other), weight(l, k, me), y_send.at[l, k], y_recv.at[l, k], {"seq": pair})

    def y_arrival(l, k):
        return remote(weight(l, k, pair), weight(l, k, pair), y_send.at[l, k], y_recv.at[l, k], {"seq": pair})

    def z_copy(l, k, side, to):
        ref = weight(l, k, slot_of(line, side))
        return remote(ref, ref, z_send.at[l, k, side, to], z_recv.at[l, k, slot_of(line, side)], {"seq": to * 2 + parity})

    def z_arrival(l, k, side, src):
        ref = weight(l, k, slot_of(src, side))
        return remote(ref, ref, z_send.at[l, k, side, src], z_recv.at[l, k, slot_of(src, side)], {"seq": pair})

    def r_copy(l, k, side, way):
        _, src, to = relays[way]
        ref = weight(l, k, slot_of(src, side))
        return remote(ref, ref, r_send.at[l, k, side, way], z_recv.at[l, k, slot_of(src, side)], {"seq": to * 2 + parity})

    def span(count, body):
        if count <= 4:
            for t in range(count):
                body(t)
        else:
            pl.loop(0, count)(body)

    def z_each(l, k, side, act):
        def body(t):
            d = reach - t

            @pl.when(line + d < lines)
            def _():
                act(z_copy(l, k, side, line + d))

            @pl.when(line >= d)
            def _():
                act(z_copy(l, k, side, line - d))

        if lines > 1:
            span(reach, body)

    def start(c):
        c.start()

    def z_start(l, k, side):
        z_each(l, k, side, start)

    def relay(l, k):
        for way, (where, src, _) in enumerate(relays):
            @pl.when(line == where)
            def _(way=way, src=src):
                for side in range(2):
                    z_arrival(l, k, side, src).wait_recv()
                    r_copy(l, k, side, way).start()

    def weights_wait(l, k):
        def body(src):
            due = src != line
            for where, taken, _ in relays:
                due = due & jnp.logical_not((line == where) & (src == taken))

            @pl.when(due)
            def _():
                for side in range(2):
                    z_arrival(l, k, side, src).wait_recv()

        span(lines, body)

    def send_next(l):
        for c in own_copies[l]:
            c.wait()
        for k in range(2):
            y_arrival(l, k).wait_recv()
        for k in range(2):
            for side in range(2):
                z_start(l, k, side)

    def ag_copy(l, p, g, h, kind, device):
        ref = xg.at[p, g, piece(h)]
        return remote(ref, ref, ag_send.at[p, g, h, kind], ag_recv.at[l, p, g, h], device)

    to_pair, to_partner = {"seq": pair}, {"grp": partner}

    def ag_wait(l, p, g, h):
        ag_copy(l, p, g, h, 0, to_pair).wait_recv()

    def ag_sends(l):
        first, second = [], []
        for j in range(1, chips):
            first.append((parity, grp, 1, 1 + j, {"grp": beside(j)}))
        first.append((parity, grp, 0, 1, to_pair))
        for j in range(1, chips):
            first.append((parity, grp, 0, 1 + j, {"grp": beside(j)}))
        first.append((parity, grp, 1, 1, to_pair))
        for h in range(2):
            first.append((parity, grp, h, 0, to_partner))
        forward = [((other, grp, 0), [(1 + j, {"grp": beside(j)}) for j in range(1, chips)])]
        for j in range(1, chips):
            forward.append(((parity, beside(j), 1), [(1, to_pair)]))
        forward.append(((other, grp, 1), []))
        for j in range(1, chips):
            forward.append(((parity, beside(j), 0), []))
        for j in range(1, chips):
            for h in range(2):
                forward.append(((other, beside(j), h), []))
        for slot, targets in forward:
            second.append((slot, [slot + t for t in targets + [(0, to_partner)]]))
        return first, second

    def ag_start(l):
        for args in ag_sends(l)[0]:
            ag_copy(l, *args).start()

    def ag_finish(l):
        first, second = ag_sends(l)
        for slot, targets in second:
            ag_wait(l, *slot)
            for args in targets:
                ag_copy(l, *args).start()
        for h in range(2):
            for p in (parity, other):
                ag_wait(l, p, partner, h)
                for j in range(1, chips):
                    ag_wait(l, p, chip_at(j) * 2 + 1 - core, h)

    def ag_drain(l):
        first, second = ag_sends(l)
        for args in first + [a for _, targets in second for a in targets]:
            ag_copy(l, *args).wait_send()

    def d_copy(l, p, x):
        return remote(part.at[p, x * 2 + 1 - core], rsd.at[p, x], d_send.at[p, x], d_recv.at[l, p, x], to_partner)

    def x_copy(l, p, j):
        return remote(
            part.at[p, beside(j), piece(0)], rx.at[p, chip], x_send.at[p, j], x_recv.at[l, p, chip], {"grp": beside(j)}
        )

    def x_arrival(l, p, j):
        ref = rx.at[p, chip_at(j)]
        return remote(ref, ref, x_send.at[p, j], x_recv.at[l, p, chip_at(j)], {"grp": beside(j)})

    def w_copy(l, j):
        x = chip_at(j)
        return remote(part.at[other, beside(j), piece(1)], ry.at[x], w_send.at[x], w_recv.at[l, x], to_pair)

    def u_copy(l):
        return remote(ub, ru, u_send.at[0], u_recv.at[l], to_pair)

    def v_copy(l, j):
        return remote(vb.at[chip_at(j)], rv.at[chip], v_send.at[j], v_recv.at[l, chip], {"grp": beside(j)})

    def v_arrival(l, j):
        ref = rv.at[chip_at(j)]
        return remote(ref, ref, v_send.at[j], v_recv.at[l, chip_at(j)], {"grp": beside(j)})

    def line_copy(l, step):
        return remote(
            st_send.at[l], st_line.at[l, line], l_send.at[l, step], l_recv.at[l, line], {"seq": (line + step) * 2 + parity}
        )

    def line_arrival(l, step):
        src = line - step
        return remote(st_send.at[l], st_line.at[l, src], l_send.at[l, step], l_recv.at[l, src], {"seq": src * 2 + parity})

    for k in range(2):
        y_copy(0, k).start()
    for c in own_copies[0]:
        c.wait()
    z_start(0, 0, 0)
    own_hidden.wait()
    ag_start(0)
    y_arrival(0, 0).wait_recv()
    z_start(0, 0, 1)
    z_start(0, 1, 0)
    y_arrival(0, 1).wait_recv()
    z_start(0, 1, 1)

    scale = head ** (-0.25)
    inv = 1.0 / math.sqrt(feats)

    def features(u, terms):
        mixed = jnp.dot(u, terms, preferred_element_type=f32)
        mixed = (mixed[:, 2 * feats :] + mixed[:, feats : 2 * feats]) + mixed[:, :feats]
        w0 = u.astype(f32) * scale
        energy = 0.5 * jnp.sum(w0 * w0, axis=-1, keepdims=True)
        return (jnp.exp(mixed - energy - stabilizer) * inv).astype(bf16)

    for l in range(layers):
        last = l == layers - 1
        ag_finish(l)
        if l == 0:
            for n in range(1, layers):
                for k in range(2):
                    y_copy(n, k).start()

        @pl.loop(0, 2 * tokens // step_rows)
        def _(t):
            at = pl.ds(pl.multiple_of(t * step_rows, step_rows), step_rows)
            b = t // (tokens // step_rows)
            src = pl.ds(pl.multiple_of(t % (tokens // step_rows) * step_rows, step_rows), step_rows)
            wide = [xg[b, g, src, :].astype(f32) for g in range(n_grp)]
            total = sum(jnp.sum(v * v, axis=-1, keepdims=True) for v in wide)
            rms = lax.rsqrt(total / (width * n_grp) + 1e-05)
            for g in range(n_grp):
                cut = slice(g * width, (g + 1) * width)
                normed[at, cut] = (wide[g] * rms * norm_gain[l : l + 1, cut]).astype(bf16)

        ag_drain(l)
        relay(l, 0)
        middle = 0 < l < layers - 1
        if middle:
            relay(l, 1)
            send_next(l + 1)
        weights_wait(l, 0)

        @pl.loop(0, 2 * mine)
        def _(i):
            h, b = i // 2, i % 2
            at = pl.ds(pl.multiple_of(h * 3 * head, 128), 3 * head)
            w = wq[l, :, :, at].reshape(n_seq * rows, 3 * head)
            x = normed[pl.ds(pl.multiple_of(b * tokens, tokens), tokens), :]
            qkv = jnp.dot(x, w, preferred_element_type=f32).astype(bf16)
            terms = proj[l, parity * mine + h]
            key = features(qkv[:, head : 2 * head], terms)
            value = qkv[:, 2 * head :]
            qf[i] = features(qkv[:, :head], terms)
            kf[i] = key
            vf[i] = value
            own_state[i, :feats] = lax.dot_general(key, value, (((0,), (0,)), ((), ())), preferred_element_type=f32)
            own_state[i, feats:] = jnp.dot(jnp.ones((16, tokens), bf16), key, preferred_element_type=f32)

        for h in range(mine):
            st_send[l, h] = (own_state[2 * h] + own_state[2 * h + 1]).astype(bf16)

        def send_state(t):
            @pl.when(line + t + 1 < lines)
            def _():
                line_copy(l, t + 1).start()

        span(lines - 1, send_state)
        if not middle:
            relay(l, 1)
            if not last:
                send_next(l + 1)

        @pl.loop(0, 2 * mine)
        def _(i):
            scores = lax.dot_general(qf[i], kf[i], (((1,), (1,)), ((), ())), preferred_element_type=f32)
            r = lax.broadcasted_iota(jnp.int32, (tokens, tokens), 0)
            c = lax.broadcasted_iota(jnp.int32, (tokens, tokens), 1)
            masked = jnp.where(r >= c, scores, 0.0)
            den[i] = jnp.broadcast_to(jnp.sum(masked, axis=-1, keepdims=True), (tokens, head))
            num[i] = jnp.dot(masked.astype(bf16), vf[i], preferred_element_type=f32)

        for h in range(mine):
            prefix[h] = jnp.zeros_like(prefix[h])

        def take_state(t):
            step = t + 1

            @pl.when(line >= step)
            def _():
                line_arrival(l, step).wait_recv()
                for h in range(mine):
                    prefix[h] = prefix[h] + st_line[l, line - step, h].astype(f32)

        span(lines - 1, take_state)

        @pl.loop(0, 2 * mine)
        def _(i):
            h, b = i // 2, i % 2
            before = prefix[h] + own_state[2 * h] * jnp.where(b == 1, 1.0, 0.0)
            q = qf[i]
            d = den[i] + jnp.sum(q.astype(f32) * before[feats : feats + 1], axis=-1, keepdims=True)
            n = num[i] + jnp.dot(q, before[:feats].astype(bf16), preferred_element_type=f32)
            a = n / d
            norm = lax.rsqrt(jnp.mean(a * a, axis=-1, keepdims=True) + 1e-06)
            to_rows = pl.ds(pl.multiple_of(b * tokens, tokens), tokens)
            to_cols = pl.ds(pl.multiple_of(h * head, 128), head)
            att[to_rows, to_cols] = (a * norm * out_gain[l, parity * mine + h]).astype(bf16)

        weights_wait(l, 1)
        per = width // oc

        def project(p, g):
            a = att[pl.ds(pl.multiple_of(p * tokens, tokens), tokens), :]
            for i in range(per):
                part[p, g, :, i * oc : (i + 1) * oc] = jnp.dot(
                    a, wo[l, g * per + i], preferred_element_type=f32
                ).astype(bf16)

        @pl.loop(0, 2 * chips)
        def _(n):
            p = lax.rem(other + n // chips, 2)
            x = lax.rem(chip + 1 + n % chips, chips)
            project(p, x * 2 + 1 - core)
            d_copy(l, p, x).start()

        @pl.loop(0, 2 * chips)
        def _(n):
            p = lax.rem(other + n // chips, 2)
            x = lax.rem(chip + 1 + n % chips, chips)
            project(p, x * 2 + core)

        hops = list(range(1, chips)) + [0]
        for own in range(2):
            p = parity if own else other
            for j in hops:
                x = chip_at(j)
                d_copy(l, p, x).wait_recv()

                @pl.loop(0, tokens // step_rows)
                def _(t, p=p, x=x, j=j):
                    at = pl.ds(pl.multiple_of(t * step_rows, step_rows), step_rows)
                    part[p, beside(j), at, :] = (
                        part[p, beside(j), at, :].astype(f32) + rsd[p, x, at, :].astype(f32)
                    ).astype(bf16)

                if j:
                    x_copy(l, p, j).start()
                if not own:
                    w_copy(l, j).start()

        for j in range(1, chips):
            x_arrival(l, other, j).wait_recv()

        @pl.loop(0, half // step_rows)
        def _(t):
            at = pl.ds(pl.multiple_of(t * step_rows, step_rows), step_rows)
            total = part[other, grp, at, :].astype(f32)
            for j in range(1, chips):
                total = total + rx[other, chip_at(j), at, :].astype(f32)
            ub[at, :] = total.astype(bf16)

        u_copy(l).start()
        for j in hops:
            w_arrival = remote(ry.at[chip_at(j)], ry.at[chip_at(j)], w_send.at[j], w_recv.at[l, chip_at(j)], to_pair)
            w_arrival.wait_recv()
            if j:
                @pl.loop(0, half // step_rows)
                def _(t, j=j):
                    at = pl.ds(pl.multiple_of(t * step_rows, step_rows), step_rows)
                    low = pl.ds(pl.multiple_of(half + t * step_rows, step_rows), step_rows)
                    vb[chip_at(j), at, :] = (
                        part[parity, beside(j), low, :].astype(f32) + ry[chip_at(j), at, :].astype(f32)
                    ).astype(bf16)

                v_copy(l, j).start()
        for j in range(1, chips):
            x_arrival(l, parity, j).wait_recv()
        u_copy(l).wait_recv()

        def finish(at, total):
            total = (xg[parity, grp, at, :].astype(f32) + total).astype(bf16)
            if last:
                out[at, :] = total
            else:
                xg[parity, grp, at, :] = total

        @pl.loop(0, half // step_rows)
        def _(t):
            at = pl.ds(pl.multiple_of(t * step_rows, step_rows), step_rows)
            total = part[parity, grp, at, :].astype(f32) + ru[at, :].astype(f32)
            for j in range(1, chips):
                total = total + rx[parity, chip_at(j), at, :].astype(f32)
            finish(at, total)

        for j in range(1, chips):
            v_arrival(l, j).wait_recv()

        @pl.loop(0, half // step_rows)
        def _(t):
            at = pl.ds(pl.multiple_of(t * step_rows, step_rows), step_rows)
            low = pl.ds(pl.multiple_of(half + t * step_rows, step_rows), step_rows)
            total = part[parity, grp, low, :].astype(f32) + ry[chip, at, :].astype(f32)
            for j in range(1, chips):
                total = total + rv[chip_at(j), at, :].astype(f32)
            finish(low, total)

        if not last:
            ag_start(l + 1)
        for p in range(2):
            for x in range(chips):
                d_copy(l, p, x).wait_send()
            for j in range(1, chips):
                x_copy(l, p, j).wait_send()
        for j in range(chips):
            w_copy(l, j).wait_send()
        u_copy(l).wait_send()
        for j in range(1, chips):
            v_copy(l, j).wait_send()

    def wait_send(c):
        c.wait_send()

    for l in range(layers):
        for k in range(2):
            y_copy(l, k).wait_send()
            for side in range(2):
                z_each(l, k, side, wait_send)
            for way, (where, _, _) in enumerate(relays):
                @pl.when(line == where)
                def _(way=way):
                    for side in range(2):
                        r_copy(l, k, side, way).wait_send()

        def state_sent(t):
            @pl.when(line + t + 1 < lines)
            def _():
                line_copy(l, t + 1).wait_send()

        span(lines - 1, state_sent)


def local(n_seq, n_grp, hidden, qkv_weight, out_weight, projection, norm_gain, out_gain):
    layers, rows, cols = qkv_weight.shape
    depth, oc = out_weight.shape[1:]
    heads, head, feats = projection.shape[1:]
    tokens, width = hidden.shape
    lines, chips, mine, half = n_seq // 2, n_grp // 2, heads // 2, tokens // 2
    scaled = projection * head ** (-0.25)
    high = lax.reduce_precision(scaled, 8, 7)
    rest = scaled - high
    mid = lax.reduce_precision(rest, 8, 7)
    low = rest - mid
    terms = jnp.concatenate([high, mid, low], axis=-1).astype(bf16)
    gains = out_gain.reshape(layers, heads, 1, head)
    dma = pltpu.SemaphoreType.DMA
    vmem = pl.BlockSpec(memory_space=pltpu.VMEM)
    anywhere = pl.BlockSpec(memory_space=pl.ANY)
    state = (feats + 16, head)
    return pl.pallas_call(
        functools.partial(kernel, n_seq, n_grp),
        out_shape=jax.ShapeDtypeStruct((tokens, width), bf16),
        in_specs=[anywhere, anywhere, anywhere, vmem, vmem, vmem],
        out_specs=vmem,
        scratch_shapes=[
            pltpu.VMEM((layers, n_seq, rows, cols // 2), bf16),
            pltpu.VMEM((layers, n_seq, depth // 2, oc), bf16),
            pltpu.VMEM((2, n_grp, tokens, width), bf16),
            pltpu.VMEM((2, n_grp, tokens, width), bf16),
            pltpu.VMEM((2, chips, tokens, width), bf16),
            pltpu.VMEM((2, chips, half, width), bf16),
            pltpu.VMEM((chips, half, width), bf16),
            pltpu.VMEM((chips, half, width), bf16),
            pltpu.VMEM((half, width), bf16),
            pltpu.VMEM((half, width), bf16),
            pltpu.VMEM((chips, half, width), bf16),
            pltpu.VMEM((2 * tokens, n_grp * width), bf16),
            pltpu.VMEM((heads, tokens, feats), bf16),
            pltpu.VMEM((heads, tokens, feats), bf16),
            pltpu.VMEM((heads, tokens, head), bf16),
            pltpu.VMEM((heads, tokens, head), f32),
            pltpu.VMEM((heads, tokens, head), f32),
            pltpu.VMEM((2 * tokens, mine * head), bf16),
            pltpu.VMEM((heads,) + state, f32),
            pltpu.VMEM((layers, mine) + state, bf16),
            pltpu.VMEM((layers, lines, mine) + state, bf16),
            pltpu.VMEM((mine,) + state, f32),
            dma((1 + 2 * layers,)),
            dma((layers, 2, 2, lines)),
            dma((layers, 2, n_seq)),
            dma((layers, 2, 2, 2)),
            dma((layers, 2)),
            dma((layers, 2)),
            dma((layers, lines)),
            dma((layers, lines)),
            dma((2, n_grp, 2, 1 + chips)),
            dma((layers, 2, n_grp, 2)),
            dma((2, chips)),
            dma((layers, 2, chips)),
            dma((2, chips)),
            dma((layers, 2, chips)),
            dma((chips,)),
            dma((layers, chips)),
            dma((1,)),
            dma((layers,)),
            dma((chips,)),
            dma((layers, chips)),
        ],
        compiler_params=pltpu.CompilerParams(
            collective_id=0, has_side_effects=True, vmem_limit_bytes=66_000_000
        ),
    )(hidden, qkv_weight, out_weight, terms, norm_gain, gains)


def solution(mesh):
    return jax.shard_map(
        functools.partial(local, mesh.shape["seq"], mesh.shape["grp"]),
        mesh=mesh,
        in_specs=(
            P("seq", "grp"),
            P(None, "seq", "grp"),
            P(None, "grp", "seq"),
            P(None, "grp", None, None),
            P(),
            P(None, "grp"),
        ),
        out_specs=P("seq", "grp"),
        check_vma=False,
    )
```

time: 362 us -> 324 us (0.90)
  the two profiles are of different devices: /device:TPU:23 before, /device:TPU:25 now
where the time goes in v1:
time: 324 us
  Pallas kernels  319 us (98%)
    pallas_call x1, Pallas kernels, local(): pl.pallas_call(functools.partial(kernel, n_seq, n_grp), out_shape=jax.Sha...  319 us

profile of v1, /device:TPU:25, one launch (start us, length us, event | category | flops | bytes accessed | tf_op | source)
XLA Modules:
  0.0 323.9 jit_solution(11583642434707762996)
XLA Ops:
  0.0 0.0 copy-start
  0.0 1.5 reduce-precision_convert_fusion.1
  1.5 1.2 pad_maximum_fusion.proj
  2.7 0.0 copy-done
  2.7 0.6 reshape.3.out_gain
  3.3 318.7 %shard_map.64 = bf16[512,512]{1,0:T(8,128)(2,1)} custom-call(bf16[512,512]{1,0:T(8,128)(2,1)} %hidden.1, bf16[3,256,1536]{2,1,0:T(8,128)(2,1)} %qkv_w.1, bf16[3,512,256]{2,1,0:T(8,128)(2,1)} %out_w.1, bf16[3,4,128,384]{3,2,1,0:T(8,128)(2,1)} %pad_maximum_fusion.proj, f32[3,2048]{1,0:T(4,128)} %norm_gain.1, f32[3,4,1,128]{3,2,1,0:T(1,128)} %reshape.3.out_gain), custom_call_target="tpu_custom_call" | custom-call | tf_op jit(solution)/shard_map/pallas_call | solution.py:521
  322.0 1.9 copy.8
Async XLA Ops:
  0.0 2.7 copy-start

commit v2 on v1

--- a/solution.py
+++ b/solution.py
@@ -22,9 +22,9 @@
 
 def kernel(
     n_seq, n_grp, hidden, qkv_w, out_w, proj, norm_gain, out_gain, out,
-    wq, wo, xg, part, rsd, rx, ry, rv, ru, ub, vb, normed, qf, kf, vf, num, den, att,
-    own_state, st_send, st_line, prefix,
-    local_sem, z_send, z_recv, r_send, y_send, y_recv, l_send, l_recv,
+    wq, wo, sq, so, xg, part, rsd, rx, ry, rv, ru, ub, vb, normed, qf, kf, vf, num, den, att,
+    own_state, st_send, st_held, st_line, prefix,
+    local_sem, z_send, s_send, z_recv, r_send, y_send, y_recv, h_send, h_recv, l_send, m_send, l_recv, k_send, k_recv,
     ag_send, ag_recv, d_send, d_recv, x_send, x_recv, w_send, w_recv, u_send, u_recv, v_send, v_recv,
 ):
     layers, rows, cols = qkv_w.shape
@@ -74,11 +74,13 @@
 
     barrier = pltpu.get_barrier_semaphore()
     for k in range(1, lines):
-        pl.semaphore_signal(barrier, inc=1, device_id={"seq": lax.rem(line + k, lines) * 2 + parity}, device_id_type=MESH)
+        along = lax.rem(line + k, lines) * 2 + parity
+        pl.semaphore_signal(barrier, inc=1, device_id={"seq": along}, device_id_type=MESH)
+        pl.semaphore_signal(barrier, inc=1, device_id={"seq": along, "grp": partner}, device_id_type=MESH)
     pl.semaphore_signal(barrier, inc=1, device_id={"seq": pair}, device_id_type=MESH)
     for k in range(1, n_grp):
         pl.semaphore_signal(barrier, inc=1, device_id={"grp": lax.rem(grp + k, n_grp)}, device_id_type=MESH)
-    pl.semaphore_wait(barrier, lines + n_grp - 1)
+    pl.semaphore_wait(barrier, 2 * lines + n_grp - 2)
 
     reach = max(1, lines - 2)
     relays = ((lines - 2, 0, lines - 1), (1, lines - 1, 0)) if lines > 2 else ()
@@ -112,17 +114,32 @@
         else:
             pl.loop(0, count)(body)
 
-    def z_each(l, k, side, act):
+    def held(l, k, side):
+        return (so if k else sq).at[l, side]
+
+    def h_copy(l, k, side):
+        src = weight(l, k, pair) if side else own_part(l, k, parity)
+        return remote(src, held(l, k, side), h_send.at[l, k, side], h_recv.at[l, k, side], {"grp": partner})
+
+    def s_copy(l, k, side, to):
+        slot = slot_of(line, side)
+        return remote(
+            held(l, k, side), weight(l, k, slot), s_send.at[l, k, side, to], z_recv.at[l, k, slot],
+            {"seq": to * 2 + parity, "grp": partner},
+        )
+
+    def z_each(l, pieces, act):
         def body(t):
             d = reach - t
-
-            @pl.when(line + d < lines)
-            def _():
-                act(z_copy(l, k, side, line + d))
-
-            @pl.when(line >= d)
-            def _():
-                act(z_copy(l, k, side, line - d))
+            for k, side in pieces:
+                @pl.when((line + d < lines) & (core == 0))
+                def _(k=k, side=side):
+                    act(z_copy(l, k, side, line + d))
+                    act(s_copy(l, k, side, line + d))
+
+                @pl.when(line >= d)
+                def _(k=k, side=side):
+                    act(z_copy(l, k, side, line - d))
 
         if lines > 1:
             span(reach, body)
@@ -130,16 +147,25 @@
     def start(c):
         c.start()
 
-    def z_start(l, k, side):
-        z_each(l, k, side, start)
-
-    def relay(l, k):
+    def hand_over(l, k, side):
+        @pl.when(core == 1)
+        def _():
+            h_copy(l, k, side).start()
+
+    def take_over(l, k, side):
+        @pl.when(core == 0)
+        def _():
+            h_copy(l, k, side).wait_recv()
+
+    def z_start(l, *pieces):
+        z_each(l, pieces, start)
+
+    def relay(l, k, side):
         for way, (where, src, _) in enumerate(relays):
             @pl.when(line == where)
             def _(way=way, src=src):
-                for side in range(2):
-                    z_arrival(l, k, side, src).wait_recv()
-                    r_copy(l, k, side, way).start()
+                z_arrival(l, k, side, src).wait_recv()
+                r_copy(l, k, side, way).start()
 
     def weights_wait(l, k):
         def body(src):
@@ -158,10 +184,13 @@
         for c in own_copies[l]:
             c.wait()
         for k in range(2):
-            y_arrival(l, k).wait_recv()
-        for k in range(2):
             for side in range(2):
-                z_start(l, k, side)
+                take_over(l, k, side)
+        if l < layers - 1:
+            z_start(l, (0, 0), (0, 1), (1, 0), (1, 1))
+        else:
+            z_start(l, (0, 0), (0, 1))
+            z_start(l, (1, 0), (1, 1))
 
     def ag_copy(l, p, g, h, kind, device):
         ref = xg.at[p, g, piece(h)]
@@ -247,22 +276,39 @@
             st_send.at[l], st_line.at[l, line], l_send.at[l, step], l_recv.at[l, line], {"seq": (line + step) * 2 + parity}
         )
 
+    def held_copy(l, step):
+        return remote(
+            st_held.at[l], st_line.at[l, line], m_send.at[l, step], l_recv.at[l, line],
+            {"seq": (line + step) * 2 + parity, "grp": partner},
+        )
+
+    def state_copy(l):
+        return remote(st_send.at[l], st_held.at[l], k_send.at[l], k_recv.at[l], to_partner)
+
     def line_arrival(l, step):
         src = line - step
         return remote(st_send.at[l], st_line.at[l, src], l_send.at[l, step], l_recv.at[l, src], {"seq": src * 2 + parity})
 
     for k in range(2):
         y_copy(0, k).start()
+    for l in range(layers):
+        for k in range(2):
+            hand_over(l, k, 0)
     for c in own_copies[0]:
         c.wait()
-    z_start(0, 0, 0)
+    take_over(0, 0, 0)
+    z_start(0, (0, 0))
     own_hidden.wait()
     ag_start(0)
-    y_arrival(0, 0).wait_recv()
-    z_start(0, 0, 1)
-    z_start(0, 1, 0)
-    y_arrival(0, 1).wait_recv()
-    z_start(0, 1, 1)
+    for k in range(2):
+        y_arrival(0, k).wait_recv()
+        hand_over(0, k, 1)
+        if k:
+            take_over(0, 1, 0)
+            z_start(0, (1, 0))
+        take_over(0, k, 1)
+        z_start(0, (k, 1))
+    relay(0, 0, 0)
 
     scale = head ** (-0.25)
     inv = 1.0 / math.sqrt(feats)
@@ -281,6 +327,7 @@
             for n in range(1, layers):
                 for k in range(2):
                     y_copy(n, k).start()
+            relay(0, 0, 1)
 
         @pl.loop(0, 2 * tokens // step_rows)
         def _(t):
@@ -295,10 +342,15 @@
                 normed[at, cut] = (wide[g] * rms * norm_gain[l : l + 1, cut]).astype(bf16)
 
         ag_drain(l)
-        relay(l, 0)
+        if l == 0:
+            for n in range(1, layers):
+                for k in range(2):
+                    y_arrival(n, k).wait_recv()
+                    hand_over(n, k, 1)
         middle = 0 < l < layers - 1
         if middle:
-            relay(l, 1)
+            relay(l, 1, 0)
+            relay(l, 1, 1)
             send_next(l + 1)
         weights_wait(l, 0)
 
@@ -321,14 +373,28 @@
         for h in range(mine):
             st_send[l, h] = (own_state[2 * h] + own_state[2 * h + 1]).astype(bf16)
 
-        def send_state(t):
-            @pl.when(line + t + 1 < lines)
-            def _():
-                line_copy(l, t + 1).start()
-
-        span(lines - 1, send_state)
+        def send_state(copy):
+            def body(t):
+                @pl.when((line + t + 1 < lines) & (core == 1))
+                def _():
+                    copy(l, t + 1).start()
+
+            span(lines - 1, body)
+
+        @pl.when((line + 1 < lines) & (core == 0))
+        def _():
+            state_copy(l).start()
+
+        send_state(line_copy)
+
+        @pl.when((line + 1 < lines) & (core == 1))
+        def _():
+            state_copy(l).wait_recv()
+
+        send_state(held_copy)
         if not middle:
-            relay(l, 1)
+            relay(l, 1, 0)
+            relay(l, 1, 1)
             if not last:
                 send_next(l + 1)
 
@@ -391,6 +457,8 @@
             x = lax.rem(chip + 1 + n % chips, chips)
             project(p, x * 2 + core)
 
+        if not last:
+            relay(l + 1, 0, 0)
         hops = list(range(1, chips)) + [0]
         for own in range(2):
             p = parity if own else other
@@ -468,6 +536,7 @@
 
         if not last:
             ag_start(l + 1)
+            relay(l + 1, 0, 1)
         for p in range(2):
             for x in range(chips):
                 d_copy(l, p, x).wait_send()
@@ -485,8 +554,12 @@
     for l in range(layers):
         for k in range(2):
             y_copy(l, k).wait_send()
-            for side in range(2):
-                z_each(l, k, side, wait_send)
+            z_each(l, ((k, 0), (k, 1)), wait_send)
+
+            @pl.when(core == 1)
+            def _(k=k):
+                for side in range(2):
+                    h_copy(l, k, side).wait_send()
             for way, (where, _, _) in enumerate(relays):
                 @pl.when(line == where)
                 def _(way=way):
@@ -494,11 +567,16 @@
                         r_copy(l, k, side, way).wait_send()
 
         def state_sent(t):
-            @pl.when(line + t + 1 < lines)
+            @pl.when((line + t + 1 < lines) & (core == 1))
             def _():
                 line_copy(l, t + 1).wait_send()
+                held_copy(l, t + 1).wait_send()
 
         span(lines - 1, state_sent)
+
+        @pl.when((line + 1 < lines) & (core == 0))
+        def _():
+            state_copy(l).wait_send()
 
 
 def local(n_seq, n_grp, hidden, qkv_weight, out_weight, projection, norm_gain, out_gain):
@@ -526,6 +604,8 @@
         scratch_shapes=[
             pltpu.VMEM((layers, n_seq, rows, cols // 2), bf16),
             pltpu.VMEM((layers, n_seq, depth // 2, oc), bf16),
+            pltpu.VMEM((layers, 2, rows, cols // 2), bf16),
+            pltpu.VMEM((layers, 2, depth // 2, oc), bf16),
             pltpu.VMEM((2, n_grp, tokens, width), bf16),
             pltpu.VMEM((2, n_grp, tokens, width), bf16),
             pltpu.VMEM((2, chips, tokens, width), bf16),
@@ -544,16 +624,23 @@
             pltpu.VMEM((2 * tokens, mine * head), bf16),
             pltpu.VMEM((heads,) + state, f32),
             pltpu.VMEM((layers, mine) + state, bf16),
+            pltpu.VMEM((layers, mine) + state, bf16),
             pltpu.VMEM((layers, lines, mine) + state, bf16),
             pltpu.VMEM((mine,) + state, f32),
             dma((1 + 2 * layers,)),
+            dma((layers, 2, 2, lines)),
             dma((layers, 2, 2, lines)),
             dma((layers, 2, n_seq)),
             dma((layers, 2, 2, 2)),
             dma((layers, 2)),
             dma((layers, 2)),
+            dma((layers, 2, 2)),
+            dma((layers, 2, 2)),
             dma((layers, lines)),
             dma((layers, lines)),
+            dma((layers, lines)),
+            dma((layers,)),
+            dma((layers,)),
             dma((2, n_grp, 2, 1 + chips)),
             dma((layers, 2, n_grp, 2)),
             dma((2, chips)),

time: 324 us -> 268 us (0.83)
  Pallas kernels: 319 us -> 263 us
    pallas_call x1, Pallas kernels: 319 us -> 263 us  [local(): pl.pallas_call(functools.partial(kernel, n_seq, n_grp), out_shape=jax.Sha...]
where the time goes in v2:
time: 268 us
  Pallas kernels  263 us (98%)
    pallas_call x1, Pallas kernels, local(): pl.pallas_call(functools.partial(kernel, n_seq, n_grp), out_shape=jax.Sha...  263 us

profile of v2, /device:TPU:25, one launch (start us, length us, event | category | flops | bytes accessed | tf_op | source)
XLA Modules:
  0.0 268.2 jit_solution(4409507937899644611)
XLA Ops:
  0.0 0.0 copy-start
  0.0 1.5 reduce-precision_convert_fusion.1
  1.5 1.2 pad_maximum_fusion.proj
  2.7 0.0 copy-done
  2.7 0.6 reshape.3.out_gain
  3.3 263.0 %shard_map.64 = bf16[512,512]{1,0:T(8,128)(2,1)} custom-call(bf16[512,512]{1,0:T(8,128)(2,1)} %hidden.1, bf16[3,256,1536]{2,1,0:T(8,128)(2,1)} %qkv_w.1, bf16[3,512,256]{2,1,0:T(8,128)(2,1)} %out_w.1, bf16[3,4,128,384]{3,2,1,0:T(8,128)(2,1)} %pad_maximum_fusion.proj, f32[3,2048]{1,0:T(4,128)} %norm_gain.1, f32[3,4,1,128]{3,2,1,0:T(1,128)} %reshape.3.out_gain), custom_call_target="tpu_custom_call" | custom-call | tf_op jit(solution)/shard_map/pallas_call | solution.py:599
  266.3 1.9 copy.8
Async XLA Ops:
  0.0 2.7 copy-start

commit v3 on v1

--- a/solution.py
+++ b/solution.py
@@ -23,15 +23,15 @@
 def kernel(
     n_seq, n_grp, hidden, qkv_w, out_w, proj, norm_gain, out_gain, out,
     wq, wo, xg, part, rsd, rx, ry, rv, ru, ub, vb, normed, qf, kf, vf, num, den, att,
-    own_state, st_send, st_line, prefix,
-    local_sem, z_send, z_recv, r_send, y_send, y_recv, l_send, l_recv,
+    proj_f, terms, own_state, st_send, st_held, st_in, st_out, st_give, prefix,
+    local_sem, z_send, z_recv, r_send, y_send, y_recv, l_send, l_recv, m_send, m_recv, k_send, k_recv,
     ag_send, ag_recv, d_send, d_recv, x_send, x_recv, w_send, w_recv, u_send, u_recv, v_send, v_recv,
 ):
     layers, rows, cols = qkv_w.shape
     depth, oc = out_w.shape[1:]
     tokens, width = hidden.shape
     heads, head = proj.shape[1:3]
-    feats = proj.shape[3] // 3
+    feats = proj.shape[3]
     lines = n_seq // 2
     chips = n_grp // 2
     mine = heads // 2
@@ -68,6 +68,8 @@
     ]
     own_hidden = pltpu.make_async_copy(hidden, xg.at[parity, grp], local_sem.at[0])
     own_hidden.start()
+    own_proj = pltpu.make_async_copy(proj.at[:, pl.ds(parity * mine, mine)], proj_f, local_sem.at[1 + 2 * layers])
+    own_proj.start()
     for both in own_copies:
         for c in both:
             c.start()
@@ -80,9 +82,6 @@
         pl.semaphore_signal(barrier, inc=1, device_id={"grp": lax.rem(grp + k, n_grp)}, device_id_type=MESH)
     pl.semaphore_wait(barrier, lines + n_grp - 1)
 
-    reach = max(1, lines - 2)
-    relays = ((lines - 2, 0, lines - 1), (1, lines - 1, 0)) if lines > 2 else ()
-
     def slot_of(where, side):
         return where * 2 + (other if side else parity)
 
@@ -92,18 +91,21 @@
     def y_arrival(l, k):
         return remote(weight(l, k, pair), weight(l, k, pair), y_send.at[l, k], y_recv.at[l, k], {"seq": pair})
 
-    def z_copy(l, k, side, to):
+    def z_copy(l, k, side, way):
         ref = weight(l, k, slot_of(line, side))
-        return remote(ref, ref, z_send.at[l, k, side, to], z_recv.at[l, k, slot_of(line, side)], {"seq": to * 2 + parity})
+        to = line - 1 if way else line + 1
+        return remote(ref, ref, z_send.at[l, k, side, way], z_recv.at[l, k, slot_of(line, side)], {"seq": to * 2 + parity})
 
     def z_arrival(l, k, side, src):
         ref = weight(l, k, slot_of(src, side))
-        return remote(ref, ref, z_send.at[l, k, side, src], z_recv.at[l, k, slot_of(src, side)], {"seq": pair})
-
-    def r_copy(l, k, side, way):
-        _, src, to = relays[way]
+        return remote(ref, ref, z_send.at[l, k, side, 0], z_recv.at[l, k, slot_of(src, side)], {"seq": pair})
+
+    def r_copy(l, k, side, hop, way):
+        src, to = (line + hop, line - 1) if way else (line - hop, line + 1)
         ref = weight(l, k, slot_of(src, side))
-        return remote(ref, ref, r_send.at[l, k, side, way], z_recv.at[l, k, slot_of(src, side)], {"seq": to * 2 + parity})
+        return remote(
+            ref, ref, r_send.at[l, k, side, way, hop], z_recv.at[l, k, slot_of(src, side)], {"seq": to * 2 + parity}
+        )
 
     def span(count, body):
         if count <= 4:
@@ -112,56 +114,74 @@
         else:
             pl.loop(0, count)(body)
 
-    def z_each(l, k, side, act):
-        def body(t):
-            d = reach - t
-
-            @pl.when(line + d < lines)
-            def _():
-                act(z_copy(l, k, side, line + d))
-
-            @pl.when(line >= d)
-            def _():
-                act(z_copy(l, k, side, line - d))
-
-        if lines > 1:
-            span(reach, body)
+    def z_up(act, l, *pieces):
+        @pl.when(line + 1 < lines)
+        def _():
+            for k, side in pieces:
+                act(z_copy(l, k, side, 0))
+
+    def z_down(act, l, *pieces):
+        @pl.when(line >= 1)
+        def _():
+            for k, side in pieces:
+                act(z_copy(l, k, side, 1))
 
     def start(c):
         c.start()
 
-    def z_start(l, k, side):
-        z_each(l, k, side, start)
-
-    def relay(l, k):
-        for way, (where, src, _) in enumerate(relays):
-            @pl.when(line == where)
-            def _(way=way, src=src):
-                for side in range(2):
-                    z_arrival(l, k, side, src).wait_recv()
-                    r_copy(l, k, side, way).start()
+    def z_start(l, *pieces):
+        z_up(start, l, *pieces)
+        z_down(start, l, *pieces)
+
+    upper = 2 * line >= lines
+
+    def r_each(hop, act, where=None):
+        up, down = (line >= hop) & (line + 1 < lines), (line + hop < lines) & (line >= 1)
+        if where is not None:
+            up, down = up & (upper == where), down & (upper != where)
+
+        @pl.when(up)
+        def _():
+            act(line - hop, 0)
+
+        @pl.when(down)
+        def _():
+            act(line + hop, 1)
+
+    def forward(l, k, hop, where=None):
+        for side in range(2):
+            def act(src, way, side=side):
+                z_arrival(l, k, side, src).wait_recv()
+                r_copy(l, k, side, hop, way).start()
+
+            r_each(hop, act, where)
+
+    def outward(l, *kinds):
+        for k in kinds:
+            forward(l, k, 1, True)
+
+    def inward(l, *kinds):
+        for k in kinds:
+            forward(l, k, 1, False)
+
+    def far(l, *kinds):
+        for k in kinds:
+            span(lines - 3, lambda t: forward(l, k, t + 2))
 
     def weights_wait(l, k):
         def body(src):
-            due = src != line
-            for where, taken, _ in relays:
-                due = due & jnp.logical_not((line == where) & (src == taken))
-
-            @pl.when(due)
+            @pl.when((src != line) & ((line == 0) | (line == lines - 1)))
             def _():
                 for side in range(2):
                     z_arrival(l, k, side, src).wait_recv()
 
         span(lines, body)
 
-    def send_next(l):
+    def prepare(l):
         for c in own_copies[l]:
             c.wait()
         for k in range(2):
             y_arrival(l, k).wait_recv()
-        for k in range(2):
-            for side in range(2):
-                z_start(l, k, side)
 
     def ag_copy(l, p, g, h, kind, device):
         ref = xg.at[p, g, piece(h)]
@@ -242,27 +262,60 @@
         ref = rv.at[chip_at(j)]
         return remote(ref, ref, v_send.at[j], v_recv.at[l, chip_at(j)], {"grp": beside(j)})
 
-    def line_copy(l, step):
-        return remote(
-            st_send.at[l], st_line.at[l, line], l_send.at[l, step], l_recv.at[l, line], {"seq": (line + step) * 2 + parity}
-        )
-
-    def line_arrival(l, step):
-        src = line - step
-        return remote(st_send.at[l], st_line.at[l, src], l_send.at[l, step], l_recv.at[l, src], {"seq": src * 2 + parity})
+    def state_copy(l):
+        return remote(st_send.at[l], st_held.at[l], k_send.at[l], k_recv.at[l], to_partner)
+
+    def chain_copy(l):
+        return remote(st_out.at[l], st_in.at[l], l_send.at[l], l_recv.at[l], {"seq": line * 2 + 2 + parity})
+
+    def give_copy(l):
+        return remote(st_in.at[l, 0], st_give.at[l], m_send.at[l], m_recv.at[l], to_partner)
+
+    below, above = line >= 1, line + 1 < lines
+
+    def wait_send(c):
+        c.wait_send()
+
+    def drain(l):
+        for k in range(2):
+            y_copy(l, k).wait_send()
+            z_up(wait_send, l, (k, 0), (k, 1))
+            z_down(wait_send, l, (k, 0), (k, 1))
+            for side in range(2):
+                def forwarded(t, k=k, side=side):
+                    r_each(t + 1, lambda src, way: r_copy(l, k, side, t + 1, way).wait_send())
+
+                span(lines - 2, forwarded)
+
+        @pl.when(above & (core == 0))
+        def _():
+            state_copy(l).wait_send()
+
+        @pl.when(above & (core == 1))
+        def _():
+            chain_copy(l).wait_send()
+
+        @pl.when(below & (core == 1))
+        def _():
+            give_copy(l).wait_send()
 
     for k in range(2):
         y_copy(0, k).start()
     for c in own_copies[0]:
         c.wait()
-    z_start(0, 0, 0)
+    z_start(0, (0, 0))
     own_hidden.wait()
     ag_start(0)
+    if layers > 1:
+        for k in range(2):
+            y_copy(1, k).start()
     y_arrival(0, 0).wait_recv()
-    z_start(0, 0, 1)
-    z_start(0, 1, 0)
+    z_start(0, (0, 1))
     y_arrival(0, 1).wait_recv()
-    z_start(0, 1, 1)
+    z_start(0, (1, 0), (1, 1))
+    for k in range(2):
+        outward(0, k)
+        inward(0, k)
 
     scale = head ** (-0.25)
     inv = 1.0 / math.sqrt(feats)
@@ -278,9 +331,12 @@
         last = l == layers - 1
         ag_finish(l)
         if l == 0:
-            for n in range(1, layers):
+            for n in range(2, layers):
                 for k in range(2):
                     y_copy(n, k).start()
+        elif last:
+            outward(l, 1)
+            inward(l, 1)
 
         @pl.loop(0, 2 * tokens // step_rows)
         def _(t):
@@ -295,11 +351,32 @@
                 normed[at, cut] = (wide[g] * rms * norm_gain[l : l + 1, cut]).astype(bf16)
 
         ag_drain(l)
-        relay(l, 0)
-        middle = 0 < l < layers - 1
-        if middle:
-            relay(l, 1)
-            send_next(l + 1)
+        if l == 0:
+            far(0, 0, 1)
+        split = l + 1 == layers - 1
+        early = ((0, 0), (0, 1)) if split else ((0, 0), (0, 1), (1, 0), (1, 1))
+        if not last:
+            prepare(l + 1)
+            z_down(start, l + 1, *early)
+
+            @pl.when(core == 0)
+            def _():
+                z_up(start, l + 1, *early)
+
+        if l == 0:
+            own_proj.wait()
+
+            @pl.loop(0, layers * mine)
+            def _(i):
+                n, h = i // mine, i % mine
+                scaled = proj_f[n, h] * scale
+                high = scaled.astype(bf16)
+                rest = scaled - high.astype(f32)
+                mid = rest.astype(bf16)
+                terms[n, h, :, :feats] = high
+                terms[n, h, :, feats : 2 * feats] = mid
+                terms[n, h, :, 2 * feats :] = (rest - mid.astype(f32)).astype(bf16)
+
         weights_wait(l, 0)
 
         @pl.loop(0, 2 * mine)
@@ -309,10 +386,10 @@
             w = wq[l, :, :, at].reshape(n_seq * rows, 3 * head)
             x = normed[pl.ds(pl.multiple_of(b * tokens, tokens), tokens), :]
             qkv = jnp.dot(x, w, preferred_element_type=f32).astype(bf16)
-            terms = proj[l, parity * mine + h]
-            key = features(qkv[:, head : 2 * head], terms)
+            split_terms = terms[l, h]
+            key = features(qkv[:, head : 2 * head], split_terms)
             value = qkv[:, 2 * head :]
-            qf[i] = features(qkv[:, :head], terms)
+            qf[i] = features(qkv[:, :head], split_terms)
             kf[i] = key
             vf[i] = value
             own_state[i, :feats] = lax.dot_general(key, value, (((0,), (0,)), ((), ())), preferred_element_type=f32)
@@ -321,16 +398,16 @@
         for h in range(mine):
             st_send[l, h] = (own_state[2 * h] + own_state[2 * h + 1]).astype(bf16)
 
-        def send_state(t):
-            @pl.when(line + t + 1 < lines)
-            def _():
-                line_copy(l, t + 1).start()
-
-        span(lines - 1, send_state)
-        if not middle:
-            relay(l, 1)
-            if not last:
-                send_next(l + 1)
+        @pl.when(above & (core == 0))
+        def _():
+            state_copy(l).start()
+
+        @pl.when(above & (core == 1) & (line == 0))
+        def _():
+            state_copy(l).wait_recv()
+            st_out[l, 0] = st_held[l]
+            st_out[l, 1] = st_send[l]
+            chain_copy(l).start()
 
         @pl.loop(0, 2 * mine)
         def _(i):
@@ -341,19 +418,40 @@
             den[i] = jnp.broadcast_to(jnp.sum(masked, axis=-1, keepdims=True), (tokens, head))
             num[i] = jnp.dot(masked.astype(bf16), vf[i], preferred_element_type=f32)
 
-        for h in range(mine):
-            prefix[h] = jnp.zeros_like(prefix[h])
-
-        def take_state(t):
-            step = t + 1
-
-            @pl.when(line >= step)
+        kinds = (0,) if split else (0, 1)
+        if last:
+            far(l, 1)
+
+        @pl.when(line == 0)
+        def _():
+            for h in range(mine):
+                prefix[h] = jnp.zeros_like(prefix[h])
+
+        @pl.when(below & (core == 1))
+        def _():
+            chain_copy(l).wait_recv()
+            give_copy(l).start()
+            for h in range(mine):
+                prefix[h] = st_in[l, 1, h].astype(f32)
+
+        @pl.when(below & above & (core == 1))
+        def _():
+            state_copy(l).wait_recv()
+            for h in range(mine):
+                st_out[l, 0, h] = (st_in[l, 0, h].astype(f32) + st_held[l, h].astype(f32)).astype(bf16)
+                st_out[l, 1, h] = (prefix[h] + own_state[2 * h] + own_state[2 * h + 1]).astype(bf16)
+            chain_copy(l).start()
+
+        if not last:
+            @pl.when(core == 1)
             def _():
-                line_arrival(l, step).wait_recv()
-                for h in range(mine):
-                    prefix[h] = prefix[h] + st_line[l, line - step, h].astype(f32)
-
-        span(lines - 1, take_state)
+                z_up(start, l + 1, *early)
+
+        @pl.when(below & (core == 0))
+        def _():
+            give_copy(l).wait_recv()
+            for h in range(mine):
+                prefix[h] = st_give[l, h].astype(f32)
 
         @pl.loop(0, 2 * mine)
         def _(i):
@@ -366,7 +464,8 @@
             norm = lax.rsqrt(jnp.mean(a * a, axis=-1, keepdims=True) + 1e-06)
             to_rows = pl.ds(pl.multiple_of(b * tokens, tokens), tokens)
             to_cols = pl.ds(pl.multiple_of(h * head, 128), head)
-            att[to_rows, to_cols] = (a * norm * out_gain[l, parity * mine + h]).astype(bf16)
+            to_gain = pl.ds(pl.multiple_of((parity * mine + h) * head, 128), head)
+            att[to_rows, to_cols] = (a * norm * out_gain[l : l + 1, to_gain]).astype(bf16)
 
         weights_wait(l, 1)
         per = width // oc
@@ -391,6 +490,8 @@
             x = lax.rem(chip + 1 + n % chips, chips)
             project(p, x * 2 + core)
 
+        if not last:
+            inward(l + 1, *kinds)
         hops = list(range(1, chips)) + [0]
         for own in range(2):
             p = parity if own else other
@@ -410,6 +511,11 @@
                 if not own:
                     w_copy(l, j).start()
 
+        if last:
+            for n in range(l):
+                drain(n)
+        else:
+            outward(l + 1, *kinds)
         for j in range(1, chips):
             x_arrival(l, other, j).wait_recv()
 
@@ -435,6 +541,8 @@
                     ).astype(bf16)
 
                 v_copy(l, j).start()
+        if last:
+            drain(l)
         for j in range(1, chips):
             x_arrival(l, parity, j).wait_recv()
         u_copy(l).wait_recv()
@@ -468,6 +576,9 @@
 
         if not last:
             ag_start(l + 1)
+            far(l + 1, *kinds)
+            if split:
+                z_start(l + 1, (1, 0), (1, 1))
         for p in range(2):
             for x in range(chips):
                 d_copy(l, p, x).wait_send()
@@ -479,41 +590,12 @@
         for j in range(1, chips):
             v_copy(l, j).wait_send()
 
-    def wait_send(c):
-        c.wait_send()
-
-    for l in range(layers):
-        for k in range(2):
-            y_copy(l, k).wait_send()
-            for side in range(2):
-                z_each(l, k, side, wait_send)
-            for way, (where, _, _) in enumerate(relays):
-                @pl.when(line == where)
-                def _(way=way):
-                    for side in range(2):
-                        r_copy(l, k, side, way).wait_send()
-
-        def state_sent(t):
-            @pl.when(line + t + 1 < lines)
-            def _():
-                line_copy(l, t + 1).wait_send()
-
-        span(lines - 1, state_sent)
-
-
 def local(n_seq, n_grp, hidden, qkv_weight, out_weight, projection, norm_gain, out_gain):
     layers, rows, cols = qkv_weight.shape
     depth, oc = out_weight.shape[1:]
     heads, head, feats = projection.shape[1:]
     tokens, width = hidden.shape
     lines, chips, mine, half = n_seq // 2, n_grp // 2, heads // 2, tokens // 2
-    scaled = projection * head ** (-0.25)
-    high = lax.reduce_precision(scaled, 8, 7)
-    rest = scaled - high
-    mid = lax.reduce_precision(rest, 8, 7)
-    low = rest - mid
-    terms = jnp.concatenate([high, mid, low], axis=-1).astype(bf16)
-    gains = out_gain.reshape(layers, heads, 1, head)
     dma = pltpu.SemaphoreType.DMA
     vmem = pl.BlockSpec(memory_space=pltpu.VMEM)
     anywhere = pl.BlockSpec(memory_space=pl.ANY)
@@ -521,7 +603,7 @@
     return pl.pallas_call(
         functools.partial(kernel, n_seq, n_grp),
         out_shape=jax.ShapeDtypeStruct((tokens, width), bf16),
-        in_specs=[anywhere, anywhere, anywhere, vmem, vmem, vmem],
+        in_specs=[anywhere, anywhere, anywhere, anywhere, vmem, vmem],
         out_specs=vmem,
         scratch_shapes=[
             pltpu.VMEM((layers, n_seq, rows, cols // 2), bf16),
@@ -542,18 +624,27 @@
             pltpu.VMEM((heads, tokens, head), f32),
             pltpu.VMEM((heads, tokens, head), f32),
             pltpu.VMEM((2 * tokens, mine * head), bf16),
+            pltpu.VMEM((layers, mine, head, feats), f32),
+            pltpu.VMEM((layers, mine, head, 3 * feats), bf16),
             pltpu.VMEM((heads,) + state, f32),
             pltpu.VMEM((layers, mine) + state, bf16),
-            pltpu.VMEM((layers, lines, mine) + state, bf16),
+            pltpu.VMEM((layers, mine) + state, bf16),
+            pltpu.VMEM((layers, 2, mine) + state, bf16),
+            pltpu.VMEM((layers, 2, mine) + state, bf16),
+            pltpu.VMEM((layers, mine) + state, bf16),
             pltpu.VMEM((mine,) + state, f32),
-            dma((1 + 2 * layers,)),
-            dma((layers, 2, 2, lines)),
+            dma((2 + 2 * layers,)),
+            dma((layers, 2, 2, 2)),
             dma((layers, 2, n_seq)),
-            dma((layers, 2, 2, 2)),
+            dma((layers, 2, 2, 2, lines)),
             dma((layers, 2)),
             dma((layers, 2)),
-            dma((layers, lines)),
-            dma((layers, lines)),
+            dma((layers,)),
+            dma((layers,)),
+            dma((layers,)),
+            dma((layers,)),
+            dma((layers,)),
+            dma((layers,)),
             dma((2, n_grp, 2, 1 + chips)),
             dma((layers, 2, n_grp, 2)),
             dma((2, chips)),
@@ -570,7 +661,7 @@
         compiler_params=pltpu.CompilerParams(
             collective_id=0, has_side_effects=True, vmem_limit_bytes=66_000_000
         ),
-    )(hidden, qkv_weight, out_weight, terms, norm_gain, gains)
+    )(hidden, qkv_weight, out_weight, projection, norm_gain, out_gain)
 
 
 def solution(mesh):

time: 324 us -> 243 us (0.75)
  Pallas kernels: 319 us -> 240 us
    pallas_call x1, Pallas kernels: 319 us -> 240 us  [local(): pl.pallas_call(functools.partial(kernel, n_seq, n_grp), out_shape=jax.Sha...]
where the time goes in v3:
time: 243 us; the launch traced here: 242 us
  Pallas kernels  240 us (99%)
    pallas_call x1, Pallas kernels, local(): pl.pallas_call(functools.partial(kernel, n_seq, n_grp), out_shape=jax.Sha...  240 us

profile of v3, /device:TPU:25, one launch (start us, length us, event | category | flops | bytes accessed | tf_op | source)
XLA Modules:
  0.0 241.8 jit_solution(10314278685054525379)
XLA Ops:
  0.0 239.9 %shard_map.64 = bf16[512,512]{1,0:T(8,128)(2,1)} custom-call(bf16[512,512]{1,0:T(8,128)(2,1)} %hidden.1, bf16[3,256,1536]{2,1,0:T(8,128)(2,1)} %qkv_w.1, bf16[3,512,256]{2,1,0:T(8,128)(2,1)} %out_w.1, f32[3,4,128,128]{3,2,1,0:T(8,128)} %proj.1, f32[3,2048]{1,0:T(4,128)} %norm_gain.1, f32[3,512]{1,0:T(4,128)} %out_gain.1), custom_call_target="tpu_custom_call" | custom-call | tf_op jit(solution)/shard_map/pallas_call | solution.py:603
  239.9 1.9 copy.8

commit v4 on v3

--- a/solution.py
+++ b/solution.py
@@ -57,6 +57,9 @@
     def weight(l, k, slot):
         return (wo if k else wq).at[l, slot]
 
+    def line_pair(l, k, where):
+        return (wo if k else wq).at[l, pl.ds(where * 2, 2)]
+
     def own_part(l, k, who):
         if k:
             return out_w.at[l, pl.ds(pl.multiple_of(who * (depth // 2), depth // 2), depth // 2)]
@@ -70,8 +73,8 @@
     own_hidden.start()
     own_proj = pltpu.make_async_copy(proj.at[:, pl.ds(parity * mine, mine)], proj_f, local_sem.at[1 + 2 * layers])
     own_proj.start()
-    for both in own_copies:
-        for c in both:
+    for pieces in own_copies:
+        for c in pieces:
             c.start()
 
     barrier = pltpu.get_barrier_semaphore()
@@ -91,21 +94,19 @@
     def y_arrival(l, k):
         return remote(weight(l, k, pair), weight(l, k, pair), y_send.at[l, k], y_recv.at[l, k], {"seq": pair})
 
-    def z_copy(l, k, side, way):
-        ref = weight(l, k, slot_of(line, side))
+    def z_copy(l, k, way, side=None):
+        ref = line_pair(l, k, line) if side is None else weight(l, k, slot_of(line, side))
         to = line - 1 if way else line + 1
-        return remote(ref, ref, z_send.at[l, k, side, way], z_recv.at[l, k, slot_of(line, side)], {"seq": to * 2 + parity})
-
-    def z_arrival(l, k, side, src):
-        ref = weight(l, k, slot_of(src, side))
-        return remote(ref, ref, z_send.at[l, k, side, 0], z_recv.at[l, k, slot_of(src, side)], {"seq": pair})
-
-    def r_copy(l, k, side, hop, way):
-        src, to = (line + hop, line - 1) if way else (line - hop, line + 1)
-        ref = weight(l, k, slot_of(src, side))
-        return remote(
-            ref, ref, r_send.at[l, k, side, way, hop], z_recv.at[l, k, slot_of(src, side)], {"seq": to * 2 + parity}
-        )
+        return remote(ref, ref, z_send.at[l, k, way], z_recv.at[l, k, line], {"seq": to * 2 + parity})
+
+    def z_arrival(l, k, src):
+        ref = line_pair(l, k, src)
+        return remote(ref, ref, z_send.at[l, k, 0], z_recv.at[l, k, src], {"seq": pair})
+
+    def r_copy(l, k, src, way):
+        ref = line_pair(l, k, src)
+        to = line - 1 if way else line + 1
+        return remote(ref, ref, r_send.at[l, k, src], z_recv.at[l, k, src], {"seq": to * 2 + parity})
 
     def span(count, body):
         if count <= 4:
@@ -114,24 +115,24 @@
         else:
             pl.loop(0, count)(body)
 
-    def z_up(act, l, *pieces):
+    def z_up(act, l, *kinds, side=None):
         @pl.when(line + 1 < lines)
         def _():
-            for k, side in pieces:
-                act(z_copy(l, k, side, 0))
-
-    def z_down(act, l, *pieces):
+            for k in kinds:
+                act(z_copy(l, k, 0, side))
+
+    def z_down(act, l, *kinds, side=None):
         @pl.when(line >= 1)
         def _():
-            for k, side in pieces:
-                act(z_copy(l, k, side, 1))
+            for k in kinds:
+                act(z_copy(l, k, 1, side))
 
     def start(c):
         c.start()
 
-    def z_start(l, *pieces):
-        z_up(start, l, *pieces)
-        z_down(start, l, *pieces)
+    def z_start(l, *kinds, side=None):
+        z_up(start, l, *kinds, side=side)
+        z_down(start, l, *kinds, side=side)
 
     upper = 2 * line >= lines
 
@@ -149,12 +150,11 @@
             act(line + hop, 1)
 
     def forward(l, k, hop, where=None):
-        for side in range(2):
-            def act(src, way, side=side):
-                z_arrival(l, k, side, src).wait_recv()
-                r_copy(l, k, side, hop, way).start()
-
-            r_each(hop, act, where)
+        def act(src, way):
+            z_arrival(l, k, src).wait_recv()
+            r_copy(l, k, src, way).start()
+
+        r_each(hop, act, where)
 
     def outward(l, *kinds):
         for k in kinds:
@@ -172,8 +172,7 @@
         def body(src):
             @pl.when((src != line) & ((line == 0) | (line == lines - 1)))
             def _():
-                for side in range(2):
-                    z_arrival(l, k, side, src).wait_recv()
+                z_arrival(l, k, src).wait_recv()
 
         span(lines, body)
 
@@ -183,9 +182,9 @@
         for k in range(2):
             y_arrival(l, k).wait_recv()
 
-    def ag_copy(l, p, g, h, kind, device):
+    def ag_copy(l, p, g, h, place, device):
         ref = xg.at[p, g, piece(h)]
-        return remote(ref, ref, ag_send.at[p, g, h, kind], ag_recv.at[l, p, g, h], device)
+        return remote(ref, ref, ag_send.at[place], ag_recv.at[p, g, h], device)
 
     to_pair, to_partner = {"seq": pair}, {"grp": partner}
 
@@ -193,43 +192,44 @@
         ag_copy(l, p, g, h, 0, to_pair).wait_recv()
 
     def ag_sends(l):
-        first, second = [], []
-        for j in range(1, chips):
-            first.append((parity, grp, 1, 1 + j, {"grp": beside(j)}))
-        first.append((parity, grp, 0, 1, to_pair))
-        for j in range(1, chips):
-            first.append((parity, grp, 0, 1 + j, {"grp": beside(j)}))
-        first.append((parity, grp, 1, 1, to_pair))
-        for h in range(2):
-            first.append((parity, grp, h, 0, to_partner))
-        forward = [((other, grp, 0), [(1 + j, {"grp": beside(j)}) for j in range(1, chips)])]
-        for j in range(1, chips):
-            forward.append(((parity, beside(j), 1), [(1, to_pair)]))
-        forward.append(((other, grp, 1), []))
-        for j in range(1, chips):
-            forward.append(((parity, beside(j), 0), []))
-        for j in range(1, chips):
-            for h in range(2):
-                forward.append(((other, beside(j), h), []))
-        for slot, targets in forward:
-            second.append((slot, [slot + t for t in targets + [(0, to_partner)]]))
+        across = [{"grp": beside(j)} for j in range(1, chips)]
+        own = [(1, d) for d in across] + [(0, to_pair)] + [(0, d) for d in across] + [(1, to_pair)]
+        own += [(h, to_partner) for h in range(2)]
+        passed = [((other, grp, 0), across)]
+        passed += [((parity, beside(j), 1), [to_pair]) for j in range(1, chips)]
+        passed += [((other, grp, 1), [])] + [((parity, beside(j), 0), []) for j in range(1, chips)]
+        passed += [((other, beside(j), h), []) for j in range(1, chips) for h in range(2)]
+        first = [(parity, grp, h, n, d) for n, (h, d) in enumerate(own)]
+        second, n = [], len(first)
+        for slot, targets in passed:
+            second.append((slot, [slot + (n + i, d) for i, d in enumerate(targets + [to_partner])]))
+            n += len(targets) + 1
         return first, second
 
     def ag_start(l):
         for args in ag_sends(l)[0]:
             ag_copy(l, *args).start()
 
-    def ag_finish(l):
-        first, second = ag_sends(l)
-        for slot, targets in second:
-            ag_wait(l, *slot)
-            for args in targets:
-                ag_copy(l, *args).start()
+    def ag_own(l):
+        for slot, targets in ag_sends(l)[1][: 2 * chips]:
+            ag_pass(l, slot, targets)
+        ag_beside(l, parity)
+
+    def ag_other(l):
+        for slot, targets in ag_sends(l)[1][2 * chips :]:
+            ag_pass(l, slot, targets)
+        ag_beside(l, other)
+
+    def ag_pass(l, slot, targets):
+        ag_wait(l, *slot)
+        for args in targets:
+            ag_copy(l, *args).start()
+
+    def ag_beside(l, p):
         for h in range(2):
-            for p in (parity, other):
-                ag_wait(l, p, partner, h)
-                for j in range(1, chips):
-                    ag_wait(l, p, chip_at(j) * 2 + 1 - core, h)
+            ag_wait(l, p, partner, h)
+            for j in range(1, chips):
+                ag_wait(l, p, chip_at(j) * 2 + 1 - core, h)
 
     def ag_drain(l):
         first, second = ag_sends(l)
@@ -237,30 +237,30 @@
             ag_copy(l, *args).wait_send()
 
     def d_copy(l, p, x):
-        return remote(part.at[p, x * 2 + 1 - core], rsd.at[p, x], d_send.at[p, x], d_recv.at[l, p, x], to_partner)
+        return remote(part.at[p, x * 2 + 1 - core], rsd.at[p, x], d_send.at[p, x], d_recv.at[p, x], to_partner)
 
     def x_copy(l, p, j):
         return remote(
-            part.at[p, beside(j), piece(0)], rx.at[p, chip], x_send.at[p, j], x_recv.at[l, p, chip], {"grp": beside(j)}
+            part.at[p, beside(j), piece(0)], rx.at[p, chip], x_send.at[p, j], x_recv.at[p, chip], {"grp": beside(j)}
         )
 
     def x_arrival(l, p, j):
         ref = rx.at[p, chip_at(j)]
-        return remote(ref, ref, x_send.at[p, j], x_recv.at[l, p, chip_at(j)], {"grp": beside(j)})
+        return remote(ref, ref, x_send.at[p, j], x_recv.at[p, chip_at(j)], {"grp": beside(j)})
 
     def w_copy(l, j):
         x = chip_at(j)
-        return remote(part.at[other, beside(j), piece(1)], ry.at[x], w_send.at[x], w_recv.at[l, x], to_pair)
+        return remote(part.at[other, beside(j), piece(1)], ry.at[x], w_send.at[x], w_recv.at[x], to_pair)
 
     def u_copy(l):
-        return remote(ub, ru, u_send.at[0], u_recv.at[l], to_pair)
+        return remote(ub, ru, u_send.at[0], u_recv.at[0], to_pair)
 
     def v_copy(l, j):
-        return remote(vb.at[chip_at(j)], rv.at[chip], v_send.at[j], v_recv.at[l, chip], {"grp": beside(j)})
+        return remote(vb.at[chip_at(j)], rv.at[chip], v_send.at[j], v_recv.at[chip], {"grp": beside(j)})
 
     def v_arrival(l, j):
         ref = rv.at[chip_at(j)]
-        return remote(ref, ref, v_send.at[j], v_recv.at[l, chip_at(j)], {"grp": beside(j)})
+        return remote(ref, ref, v_send.at[j], v_recv.at[chip_at(j)], {"grp": beside(j)})
 
     def state_copy(l):
         return remote(st_send.at[l], st_held.at[l], k_send.at[l], k_recv.at[l], to_partner)
@@ -272,6 +272,7 @@
         return remote(st_in.at[l, 0], st_give.at[l], m_send.at[l], m_recv.at[l], to_partner)
 
     below, above = line >= 1, line + 1 < lines
+    held_back = (core == 1) & (line == lines - 2)
 
     def wait_send(c):
         c.wait_send()
@@ -279,13 +280,13 @@
     def drain(l):
         for k in range(2):
             y_copy(l, k).wait_send()
-            z_up(wait_send, l, (k, 0), (k, 1))
-            z_down(wait_send, l, (k, 0), (k, 1))
-            for side in range(2):
-                def forwarded(t, k=k, side=side):
-                    r_each(t + 1, lambda src, way: r_copy(l, k, side, t + 1, way).wait_send())
-
-                span(lines - 2, forwarded)
+            z_up(wait_send, l, k)
+            z_down(wait_send, l, k)
+
+            def forwarded(t, k=k):
+                r_each(t + 1, lambda src, way: r_copy(l, k, src, way).wait_send())
+
+            span(lines - 2, forwarded)
 
         @pl.when(above & (core == 0))
         def _():
@@ -303,16 +304,16 @@
         y_copy(0, k).start()
     for c in own_copies[0]:
         c.wait()
-    z_start(0, (0, 0))
+    z_start(0, 0, side=0)
     own_hidden.wait()
     ag_start(0)
     if layers > 1:
         for k in range(2):
             y_copy(1, k).start()
     y_arrival(0, 0).wait_recv()
-    z_start(0, (0, 1))
+    z_start(0, 0, side=1)
     y_arrival(0, 1).wait_recv()
-    z_start(0, (1, 0), (1, 1))
+    z_start(0, 1)
     for k in range(2):
         outward(0, k)
         inward(0, k)
@@ -329,7 +330,21 @@
 
     for l in range(layers):
         last = l == layers - 1
-        ag_finish(l)
+        def normalize(b):
+            @pl.loop(0, tokens // step_rows)
+            def _(t):
+                at = pl.ds(pl.multiple_of(b * tokens + t * step_rows, step_rows), step_rows)
+                src = pl.ds(pl.multiple_of(t * step_rows, step_rows), step_rows)
+                wide = [xg[b, g, src, :].astype(f32) for g in range(n_grp)]
+                total = sum(jnp.sum(v * v, axis=-1, keepdims=True) for v in wide)
+                rms = lax.rsqrt(total / (width * n_grp) + 1e-05)
+                for g in range(n_grp):
+                    cut = slice(g * width, (g + 1) * width)
+                    normed[at, cut] = (wide[g] * rms * norm_gain[l : l + 1, cut]).astype(bf16)
+
+        ag_own(l)
+        normalize(parity)
+        ag_other(l)
         if l == 0:
             for n in range(2, layers):
                 for k in range(2):
@@ -337,29 +352,17 @@
         elif last:
             outward(l, 1)
             inward(l, 1)
-
-        @pl.loop(0, 2 * tokens // step_rows)
-        def _(t):
-            at = pl.ds(pl.multiple_of(t * step_rows, step_rows), step_rows)
-            b = t // (tokens // step_rows)
-            src = pl.ds(pl.multiple_of(t % (tokens // step_rows) * step_rows, step_rows), step_rows)
-            wide = [xg[b, g, src, :].astype(f32) for g in range(n_grp)]
-            total = sum(jnp.sum(v * v, axis=-1, keepdims=True) for v in wide)
-            rms = lax.rsqrt(total / (width * n_grp) + 1e-05)
-            for g in range(n_grp):
-                cut = slice(g * width, (g + 1) * width)
-                normed[at, cut] = (wide[g] * rms * norm_gain[l : l + 1, cut]).astype(bf16)
-
+        normalize(other)
         ag_drain(l)
         if l == 0:
             far(0, 0, 1)
         split = l + 1 == layers - 1
-        early = ((0, 0), (0, 1)) if split else ((0, 0), (0, 1), (1, 0), (1, 1))
+        early = (0,) if split else (0, 1)
         if not last:
             prepare(l + 1)
             z_down(start, l + 1, *early)
 
-            @pl.when(core == 0)
+            @pl.when(jnp.logical_not(held_back))
             def _():
                 z_up(start, l + 1, *early)
 
@@ -420,7 +423,9 @@
 
         kinds = (0,) if split else (0, 1)
         if last:
-            far(l, 1)
+            @pl.when(jnp.logical_not(held_back))
+            def _():
+                far(l, 1)
 
         @pl.when(line == 0)
         def _():
@@ -443,9 +448,13 @@
             chain_copy(l).start()
 
         if not last:
-            @pl.when(core == 1)
+            @pl.when(held_back)
             def _():
                 z_up(start, l + 1, *early)
+        else:
+            @pl.when(held_back)
+            def _():
+                far(l, 1)
 
         @pl.when(below & (core == 0))
         def _():
@@ -529,7 +538,7 @@
 
         u_copy(l).start()
         for j in hops:
-            w_arrival = remote(ry.at[chip_at(j)], ry.at[chip_at(j)], w_send.at[j], w_recv.at[l, chip_at(j)], to_pair)
+            w_arrival = remote(ry.at[chip_at(j)], ry.at[chip_at(j)], w_send.at[j], w_recv.at[chip_at(j)], to_pair)
             w_arrival.wait_recv()
             if j:
                 @pl.loop(0, half // step_rows)
@@ -548,11 +557,10 @@
         u_copy(l).wait_recv()
 
         def finish(at, total):
-            total = (xg[parity, grp, at, :].astype(f32) + total).astype(bf16)
-            if last:
-                out[at, :] = total
-            else:
-                xg[parity, grp, at, :] = total
+            xg[parity, grp, at, :] = (xg[parity, grp, at, :].astype(f32) + total).astype(bf16)
+
+        def result(h):
+            return pltpu.make_async_copy(xg.at[parity, grp, piece(h)], out.at[piece(h)], local_sem.at[2 + 2 * layers + h])
 
         @pl.loop(0, half // step_rows)
         def _(t):
@@ -562,6 +570,8 @@
                 total = total + rx[parity, chip_at(j), at, :].astype(f32)
             finish(at, total)
 
+        if last:
+            result(0).start()
         for j in range(1, chips):
             v_arrival(l, j).wait_recv()
 
@@ -574,11 +584,13 @@
                 total = total + rv[chip_at(j), at, :].astype(f32)
             finish(low, total)
 
-        if not last:
+        if last:
+            result(1).start()
+        else:
             ag_start(l + 1)
             far(l + 1, *kinds)
             if split:
-                z_start(l + 1, (1, 0), (1, 1))
+                z_start(l + 1, 1)
         for p in range(2):
             for x in range(chips):
                 d_copy(l, p, x).wait_send()
@@ -589,6 +601,10 @@
         u_copy(l).wait_send()
         for j in range(1, chips):
             v_copy(l, j).wait_send()
+        if last:
+            for h in range(2):
+                result(h).wait()
+
 
 def local(n_seq, n_grp, hidden, qkv_weight, out_weight, projection, norm_gain, out_gain):
     layers, rows, cols = qkv_weight.shape
@@ -604,7 +620,7 @@
         functools.partial(kernel, n_seq, n_grp),
         out_shape=jax.ShapeDtypeStruct((tokens, width), bf16),
         in_specs=[anywhere, anywhere, anywhere, anywhere, vmem, vmem],
-        out_specs=vmem,
+        out_specs=anywhere,
         scratch_shapes=[
             pltpu.VMEM((layers, n_seq, rows, cols // 2), bf16),
             pltpu.VMEM((layers, n_seq, depth // 2, oc), bf16),
@@ -633,10 +649,10 @@
             pltpu.VMEM((layers, 2, mine) + state, bf16),
             pltpu.VMEM((layers, mine) + state, bf16),
             pltpu.VMEM((mine,) + state, f32),
-            dma((2 + 2 * layers,)),
-            dma((layers, 2, 2, 2)),
-            dma((layers, 2, n_seq)),
-            dma((layers, 2, 2, 2, lines)),
+            dma((4 + 2 * layers,)),
+            dma((layers, 2, 2)),
+            dma((layers, 2, lines)),
+            dma((layers, 2, lines)),
             dma((layers, 2)),
             dma((layers, 2)),
             dma((layers,)),
@@ -645,18 +661,18 @@
             dma((layers,)),
             dma((layers,)),
             dma((layers,)),
-            dma((2, n_grp, 2, 1 + chips)),
-            dma((layers, 2, n_grp, 2)),
+            dma((8 * chips - 2,)),
+            dma((2, n_grp, 2)),
             dma((2, chips)),
-            dma((layers, 2, chips)),
             dma((2, chips)),
-            dma((layers, 2, chips)),
+            dma((2, chips)),
+            dma((2, chips)),
             dma((chips,)),
-            dma((layers, chips)),
+            dma((chips,)),
             dma((1,)),
-            dma((layers,)),
+            dma((1,)),
             dma((chips,)),
-            dma((layers, chips)),
+            dma((chips,)),
         ],
         compiler_params=pltpu.CompilerParams(
             collective_id=0, has_side_effects=True, vmem_limit_bytes=66_000_000

time: 243 us -> 241 us (level)
  no operation moved by 1% of the time
where the time goes in v4:
time: 241 us; the launch traced here: 240 us
  Pallas kernels  239 us (99%)
    pallas_call x1, Pallas kernels, local(): pl.pallas_call(functools.partial(kernel, n_seq, n_grp), out_shape=jax.Sha...  239 us

profile of v4, /device:TPU:25, one launch (start us, length us, event | category | flops | bytes accessed | tf_op | source)
XLA Modules:
  0.0 240.4 jit_solution(15104718008337123120)
XLA Ops:
  0.0 238.5 %shard_map.64 = bf16[512,512]{1,0:T(8,128)(2,1)} custom-call(bf16[512,512]{1,0:T(8,128)(2,1)} %hidden.1, bf16[3,256,1536]{2,1,0:T(8,128)(2,1)} %qkv_w.1, bf16[3,512,256]{2,1,0:T(8,128)(2,1)} %out_w.1, f32[3,4,128,128]{3,2,1,0:T(8,128)} %proj.1, f32[3,2048]{1,0:T(4,128)} %norm_gain.1, f32[3,512]{1,0:T(4,128)} %out_gain.1), custom_call_target="tpu_custom_call" | custom-call | tf_op jit(solution)/shard_map/pallas_call | solution.py:619
  238.5 1.9 copy.8

commit v5 on v4

--- a/solution.py
+++ b/solution.py
@@ -70,12 +70,12 @@
         for l in range(layers)
     ]
     own_hidden = pltpu.make_async_copy(hidden, xg.at[parity, grp], local_sem.at[0])
+    for pieces in own_copies:
+        for c in pieces:
+            c.start()
     own_hidden.start()
     own_proj = pltpu.make_async_copy(proj.at[:, pl.ds(parity * mine, mine)], proj_f, local_sem.at[1 + 2 * layers])
     own_proj.start()
-    for pieces in own_copies:
-        for c in pieces:
-            c.start()
 
     barrier = pltpu.get_barrier_semaphore()
     for k in range(1, lines):
@@ -305,6 +305,7 @@
     for c in own_copies[0]:
         c.wait()
     z_start(0, 0, side=0)
+    z_start(0, 1, side=0)
     own_hidden.wait()
     ag_start(0)
     if layers > 1:
@@ -313,7 +314,7 @@
     y_arrival(0, 0).wait_recv()
     z_start(0, 0, side=1)
     y_arrival(0, 1).wait_recv()
-    z_start(0, 1)
+    z_start(0, 1, side=1)
     for k in range(2):
         outward(0, k)
         inward(0, k)
@@ -486,40 +487,40 @@
                     a, wo[l, g * per + i], preferred_element_type=f32
                 ).astype(bf16)
 
-        @pl.loop(0, 2 * chips)
-        def _(n):
-            p = lax.rem(other + n // chips, 2)
-            x = lax.rem(chip + 1 + n % chips, chips)
-            project(p, x * 2 + 1 - core)
-            d_copy(l, p, x).start()
-
-        @pl.loop(0, 2 * chips)
-        def _(n):
-            p = lax.rem(other + n // chips, 2)
-            x = lax.rem(chip + 1 + n % chips, chips)
-            project(p, x * 2 + core)
-
         if not last:
             inward(l + 1, *kinds)
         hops = list(range(1, chips)) + [0]
-        for own in range(2):
-            p = parity if own else other
-            for j in hops:
-                x = chip_at(j)
-                d_copy(l, p, x).wait_recv()
-
-                @pl.loop(0, tokens // step_rows)
-                def _(t, p=p, x=x, j=j):
-                    at = pl.ds(pl.multiple_of(t * step_rows, step_rows), step_rows)
-                    part[p, beside(j), at, :] = (
-                        part[p, beside(j), at, :].astype(f32) + rsd[p, x, at, :].astype(f32)
-                    ).astype(bf16)
-
-                if j:
-                    x_copy(l, p, j).start()
-                if not own:
-                    w_copy(l, j).start()
-
+
+        def make(p, j):
+            x = chip_at(j)
+            project(p, x * 2 + 1 - core)
+            d_copy(l, p, x).start()
+            project(p, beside(j))
+
+        def combine(p, j, onward):
+            x = chip_at(j)
+            d_copy(l, p, x).wait_recv()
+
+            @pl.loop(0, tokens // step_rows)
+            def _(t):
+                at = pl.ds(pl.multiple_of(t * step_rows, step_rows), step_rows)
+                part[p, beside(j), at, :] = (
+                    part[p, beside(j), at, :].astype(f32) + rsd[p, x, at, :].astype(f32)
+                ).astype(bf16)
+
+            if j:
+                x_copy(l, p, j).start()
+            if onward:
+                w_copy(l, j).start()
+
+        todo = [(other, j, True) for j in hops] + [(parity, j, False) for j in hops]
+        ahead = 2
+        for n, (p, j, onward) in enumerate(todo):
+            make(p, j)
+            if n + 1 >= ahead:
+                combine(*todo[n + 1 - ahead])
+        for n in range(len(todo) + 1 - ahead, len(todo)):
+            combine(*todo[n])
         if last:
             for n in range(l):
                 drain(n)

time: 241 us -> 238 us (0.988)
  Pallas kernels: 239 us -> 235 us
    pallas_call x1, Pallas kernels: 239 us -> 235 us  [local(): pl.pallas_call(functools.partial(kernel, n_seq, n_grp), out_shape=jax.Sha...]
where the time goes in v5:
time: 238 us; the launch traced here: 237 us
  Pallas kernels  235 us (99%)
    pallas_call x1, Pallas kernels, local(): pl.pallas_call(functools.partial(kernel, n_seq, n_grp), out_shape=jax.Sha...  235 us

profile of v5, /device:TPU:25, one launch (start us, length us, event | category | flops | bytes accessed | tf_op | source)
XLA Modules:
  0.0 237.0 jit_solution(13807971047628191597)
XLA Ops:
  0.0 235.1 %shard_map.64 = bf16[512,512]{1,0:T(8,128)(2,1)} custom-call(bf16[512,512]{1,0:T(8,128)(2,1)} %hidden.1, bf16[3,256,1536]{2,1,0:T(8,128)(2,1)} %qkv_w.1, bf16[3,512,256]{2,1,0:T(8,128)(2,1)} %out_w.1, f32[3,4,128,128]{3,2,1,0:T(8,128)} %proj.1, f32[3,2048]{1,0:T(4,128)} %norm_gain.1, f32[3,512]{1,0:T(4,128)} %out_gain.1), custom_call_target="tpu_custom_call" | custom-call | tf_op jit(solution)/shard_map/pallas_call | solution.py:620
  235.1 1.9 copy.8
